TPU v7x, 32 devices: a whole 2x2x4 slice. The times are simulated.
32 devices in a mesh: expert: 2 (over x), tensor: 16 (over z, y, core).
Axes of the slice: x: 2, y: 2, z: 4, core: 2. Of those that a mesh axis runs over, the one named last changes fastest.
Arguments:
- tokens: bfloat16 [96, 6144], P('expert', 'tensor'), may hold values from -6 to 6
- expert_ids: int32 [96, 2], P('expert'), may hold values from 0 to 1, as said below
- route_weight: int32 [96, 2], P('expert'), may hold values from 1 to 4095
- gate_weight: bfloat16 [2, 6144, 8192], P('expert', None, 'tensor'), may hold values from -0.078125 to 0.078125
- up_weight: bfloat16 [2, 6144, 8192], P('expert', None, 'tensor'), may hold values from -0.078125 to 0.078125
- down_weight: bfloat16 [2, 8192, 6144], P('expert', 'tensor'), may hold values from -0.0625 to 0.0625
Outputs:
- mixed: bfloat16 [96, 6144], P('expert', 'tensor')
- expert_load: float32 [2, 2], replicated
Inputs may be any that keep to these rules, and one draw needn't show every extreme that they name: `expert_ids`: each row names two different experts. The hot expert is the one named in the first column of the first row of every aligned block of 48 rows (the tokens of one expert group), the same in all blocks. In each block exactly 48 rows name the hot expert, in either column; every other expert is named by 7 or 48 rows of each block, and by exactly 48 rows in some.
All inputs are finite; a program needn't handle non-finite values.
Results may differ from a plain program's by a relative error of at most 0.005.
Values may be sent and summed in bfloat16 or wider, within the bound.
No kernel may reach another device: no remote copies, remote signals or barrier semaphores. Data moves between devices by JAX's collectives and lax.ppermute only.
A program may use at most 64 MiB of HBM per device.

v0:
```python
import functools

import jax
import jax.numpy as jnp
from jax import lax
from jax.experimental import pallas as pl
from jax.experimental.pallas import tpu as pltpu
from jax.sharding import PartitionSpec as P

AXES = ("expert", "tensor")
VMEM = pl.BlockSpec(memory_space=pltpu.VMEM)
LIMIT = 8 * 2**20
LANES, SUBLANES = 128, 16


def swap(value, expert_bit, tensor_mask):
    width = lax.axis_size("tensor")
    mask = expert_bit * width + tensor_mask
    pairs = [(i, i ^ mask) for i in range(2 * width)]
    return lax.ppermute(value, AXES, pairs)


def cost(flops, moved, exps=0):
    return pl.CostEstimate(flops=flops, bytes_accessed=moved, transcendentals=exps)


def route_kernel(ids, raw, mixing, stats):
    expert = lax.axis_index("expert")
    weights = raw[...].astype(jnp.float32)
    share = weights / jnp.sum(weights, axis=0, keepdims=True)
    count = share.shape[1]
    shape = (count, count)
    diagonal = lax.broadcasted_iota(jnp.int32, shape, 0) == lax.broadcasted_iota(jnp.int32, shape, 1)
    for place, label in enumerate((expert, 1 - expert)):
        row = jnp.sum(jnp.where(ids[...] == label, share, 0.0), axis=0, keepdims=True)
        mixing[:, place : place + 1] = jnp.sum(jnp.where(diagonal, row, 0.0), axis=1, keepdims=True)
    stats[...] = jnp.zeros_like(stats)
    for label in range(2):
        named = ids[...] == label
        for place, term in enumerate((jnp.where(named, 1.0, 0.0), jnp.where(named, share, 0.0))):
            total = jnp.sum(jnp.sum(term, axis=1, keepdims=True), axis=0, keepdims=True)
            stats[place : place + 1, label : label + 1] = total


def early_kernel(out):
    out[...] = jnp.zeros_like(out)


def gather_kernel(*refs):
    parts, out = refs[-1 - refs[-1].shape[0] : -1], refs[-1]
    for z, part in enumerate(parts):
        out[z] = part[...]


def crossed(z):
    return int(z > 0)


def project_kernel(zs, last, *refs):
    buffers, (gate_w, up_w), refs = refs[:8], refs[8:10], refs[10:]
    tokens, width = buffers[0].shape[1:]
    rows = refs[-1]
    here = lax.axis_index("tensor")
    pair = 2 * width
    blocks = [(flip, z) for flip in range(2) for z in zs]
    for index, buffer in enumerate(buffers):
        group, flip, hop = index // 4, index // 2 % 2, index % 2
        for slot, z in enumerate(zs):
            side = (here & 1) ^ hop ^ crossed(z)
            start = pl.multiple_of(blocks.index((flip, z)) * pair + side * width, 128)
            rows[pl.ds(group * tokens, tokens), pl.ds(start, width)] = buffer[slot]
    sums = [refs[0][...], refs[1][...]] if last else [None, None]
    for block, (flip, z) in enumerate(blocks):
        left = rows[:, block * pair : (block + 1) * pair]
        place = (here ^ (4 * z + 2 * flip)) >> 1
        span = pl.ds(pl.multiple_of(place * pair, 128), pair)
        for which, weights in enumerate((gate_w, up_w)):
            term = jnp.dot(left, weights[0, span], preferred_element_type=jnp.float32)
            sums[which] = term if sums[which] is None else sums[which] + term
    gate, up = sums
    if last:
        refs[2][...] = (gate / (1.0 + jnp.exp(-gate)) * up).astype(refs[2].dtype)
    else:
        refs[1][...], refs[2][...] = gate, up


def down_kernel(zs, hidden, weights, send, keep):
    tokens, width = keep.shape[3:]
    here = lax.axis_index("tensor")
    core = here & 1
    pair = 2 * width
    left = hidden[...]
    for flip in range(2):
        for slot, z in enumerate(zs):
            place = (here ^ (4 * z + 2 * flip)) >> 1
            span = pl.ds(pl.multiple_of(place * pair, 128), pair)
            product = jnp.dot(left, weights[0, :, span], preferred_element_type=jnp.float32)
            low, high = product[:, :width], product[:, width:]
            mine = jnp.where(core == 0, low, high)
            other = jnp.where(core == 0, high, low)
            for group in range(2):
                part = slice(group * tokens, (group + 1) * tokens)
                kept, sent = (other, mine) if crossed(z) else (mine, other)
                keep[flip, group, slot] = kept[part]
                send[flip, group, slot] = sent[part].astype(send.dtype)


def add_kernel(keep, arrived, *refs):
    *stats, own, to_x, to_y, to_xy = refs
    slots, rows = own.shape[:2]
    for slot in range(slots):
        for flip, group, out in ((1, 1, to_xy), (1, 0, to_y), (0, 0, own)):
            total = keep[flip, group, slot] + arrived[flip, group, slot].astype(jnp.float32)
            out[slot] = total.astype(out.dtype)
        total = keep[0, 1, slot] + arrived[0, 1, slot].astype(jnp.float32)
        to_x[pl.ds(slot * rows, rows)] = total.astype(to_x.dtype)
    for block in stats:
        rest = block[...]
        for part in range(3):
            rounded = rest.astype(to_x.dtype)
            to_x[pl.ds(slots * rows, SUBLANES), pl.ds(part * LANES, LANES)] = rounded
            rest = rest - rounded.astype(jnp.float32)


def mix_kernel(slots, mixing, own, from_x, from_y, from_xy, *refs):
    stats, outs, load = (refs[:1], refs[1:-1], refs[-1:]) if len(refs) > slots else ((), refs, ())
    rows = mixing.shape[0]
    mine, theirs = mixing[:, 0:1], mixing[:, 1:2]
    for slot, out in enumerate(outs):
        near = own[slot] + from_y[slot].astype(jnp.float32)
        far = from_x[pl.ds(slot * rows, rows)].astype(jnp.float32) + from_xy[slot].astype(jnp.float32)
        out[...] = (mine * near + theirs * far).astype(out.dtype)
    for here, both in zip(stats, load):
        parts = [
            from_x[pl.ds(slots * rows, SUBLANES), pl.ds(part * LANES, LANES)].astype(jnp.float32)
            for part in range(3)
        ]
        both[...] = (here[...] + (parts[0] + (parts[1] + parts[2]))) / rows


def final_kernel(load, keep, *refs):
    *parts, mixed, expert_load = refs
    total = keep[...]
    for part in parts:
        total = total + part[...].astype(jnp.float32)
    mixed[...] = total.astype(mixed.dtype)
    expert_load[...] = load[: expert_load.shape[0], : expert_load.shape[1]]


def call(kernel, outs, inputs, scratch=(), estimate=None):
    return pl.pallas_call(
        kernel,
        out_shape=outs,
        in_specs=[VMEM] * len(inputs),
        out_specs=jax.tree.map(lambda _: VMEM, outs),
        scratch_shapes=list(scratch),
        cost_estimate=estimate,
        compiler_params=pltpu.CompilerParams(vmem_limit_bytes=LIMIT),
    )(*inputs)


def dense(tokens, expert_ids, route_weight, gate_weight, up_weight, down_weight):
    rows, width = tokens.shape
    model, units = gate_weight.shape[1:]
    pieces_z = lax.axis_size("tensor") // 4
    bf16, f32 = jnp.bfloat16, jnp.float32
    shape = jax.ShapeDtypeStruct

    mixing, stats = call(
        route_kernel,
        (shape((rows, 2), f32), shape((SUBLANES, LANES), f32)),
        (expert_ids.T, route_weight.T),
    )
    sets = (range(2), range(2, pieces_z))
    along_z = [tokens, *(swap(tokens, 0, 4 * z + 1) for z in range(1, pieces_z))]
    early = call(early_kernel, shape((SUBLANES, LANES), f32), (), estimate=cost(120 * rows * model * units, 0))
    both = []
    for zs in sets:
        block = shape((len(zs), rows, width), bf16)
        own = call(gather_kernel, block, [early, *(along_z[z] for z in zs)])
        moves = [(1, 0), (1, 2), (0, 2)]
        far_x, far_xy, near_y = (swap(own, x, y) for x, y in moves)
        buffers = {"own": own, "y": near_y, "x": far_x, "xy": far_xy}
        both.append([half for one in buffers.values() for half in (one, swap(one, 0, 1))])

    halves = shape((2 * rows, units), f32)
    estimate = cost(8 * rows * model * units, 2 * model * units, 2 * rows * units)
    weights = (gate_weight, up_weight)
    first = call(
        functools.partial(project_kernel, sets[0], False),
        (halves, halves),
        (*both[0], *weights, down_weight),
        scratch=[pltpu.VMEM((2 * rows, len(sets[0]) * model // pieces_z), bf16)],
        estimate=estimate,
    )
    hidden = call(
        functools.partial(project_kernel, sets[1], True),
        shape((2 * rows, units), bf16),
        (*both[1], *weights, *first),
        scratch=[pltpu.VMEM((2 * rows, len(sets[1]) * model // pieces_z), bf16)],
        estimate=estimate,
    )

    small = shape((rows, width), bf16)
    small32 = shape((rows, width), f32)
    pieces, load = {}, None
    for name, zs in (("far", sets[1]), ("near", sets[0])):
        block = (len(zs), rows, width)
        extra = [stats] if name == "far" else []
        send, keep = call(
            functools.partial(down_kernel, zs),
            (shape((2, 2, *block), bf16), shape((2, 2, *block), f32)),
            (hidden, down_weight),
            estimate=cost(2 * rows * model * units, model * units),
        )
        arrived = swap(send, 0, 1)
        own, to_x, to_y, to_xy = call(
            add_kernel,
            (
                shape(block, f32),
                shape((len(zs) * rows + len(extra) * SUBLANES, width), bf16),
                *[shape(block, bf16)] * 2,
            ),
            (keep, arrived, *extra),
        )
        from_xy = swap(to_xy, 1, 2)
        from_x = swap(to_x, 1, 0)
        from_y = swap(to_y, 0, 2)
        outs = call(
            functools.partial(mix_kernel, len(zs)),
            [*[small if z else small32 for z in zs], *[shape((SUBLANES, LANES), f32)] * len(extra)],
            (mixing, own, from_x, from_y, from_xy, *extra),
        )
        pieces.update(zip(zs, outs))
        load = outs[-1] if extra else load
    arrived = [swap(pieces[z], 0, 4 * z + 1) for z in range(pieces_z - 1, 0, -1)]
    mixed, expert_load = call(final_kernel, (small, shape((2, 2), f32)), (load, pieces[0], *arrived))
    return (mixed, expert_load)


def swiglu(gate_value, up_value):
    return (jax.nn.silu(gate_value) * up_value).astype(jnp.bfloat16)


def matmul(left, right):
    return jnp.dot(left, right, preferred_element_type=jnp.float32)


def route_stats(id_block, raw_block, labels):
    weights = raw_block.astype(jnp.float32)
    route_share = weights / jnp.sum(weights, axis=1, keepdims=True)
    flat_chosen = (
        (id_block[:, :, None] == labels[None, None, :])
        .astype(jnp.int32)
        .reshape(-1, labels.shape[0])
    )
    chosen_float = flat_chosen.astype(jnp.float32)
    stats = jnp.stack(
        [jnp.sum(chosen_float, axis=0), jnp.sum(route_share.reshape(-1, 1) * chosen_float, axis=0)]
    )
    return (route_share, flat_chosen, stats)


def hot_inputs(hot_local, hot_id, labels):
    is_target = (labels == hot_id)[:, None, None]
    send_rows = jnp.where(is_target, hot_local[None], jnp.zeros_like(hot_local)[None])
    arrived = lax.all_to_all(send_rows, "expert", split_axis=0, concat_axis=0, tiled=True)
    return arrived.reshape(-1, hot_local.shape[1])


def general(tokens, expert_ids, route_weight, gate_weight, up_weight, down_weight):
    tok_rows = expert_ids.shape[0]
    experts = lax.axis_size("expert") * gate_weight.shape[0]
    hot_rows = tok_rows - tok_rows // 8 * min(experts - 2, 1)
    capacity = (2 * tok_rows - hot_rows + experts - 2) // (experts - 1)
    hot_id = expert_ids[0, 0]
    own_gate = gate_weight[0]
    own_up = up_weight[0]
    own_down = down_weight[0]
    hot_gate_w, hot_up_w, hot_down_w = (own_gate, own_up, own_down)
    labels = jnp.arange(experts, dtype=jnp.int32)
    route_share, flat_chosen, local_stats = route_stats(expert_ids, route_weight, labels)
    cold_chosen = flat_chosen * (labels != hot_id).astype(jnp.int32)[None, :]
    slot_index = jnp.sum((jnp.cumsum(cold_chosen, axis=0) - 1) * cold_chosen, axis=1)
    is_live = jnp.sum(cold_chosen, axis=1)
    target = jnp.sum(cold_chosen * labels[None, :], axis=1) * capacity + slot_index
    buffer_rows = jnp.arange(experts * capacity, dtype=jnp.int32)
    cold_pick = ((target[None, :] == buffer_rows[:, None]) & (is_live[None, :] == 1)).astype(
        jnp.bfloat16
    )
    cold_pick = jnp.sum(cold_pick.reshape(experts * capacity, tok_rows, 2), axis=2)
    hot_match = (expert_ids == hot_id).astype(jnp.int32)
    hot_flag = jnp.sum(hot_match, axis=1)
    hot_rank = jnp.cumsum(hot_flag) - 1
    hot_slots = jnp.arange(hot_rows, dtype=jnp.int32)
    hot_pick = ((hot_rank[None, :] == hot_slots[:, None]) & (hot_flag[None, :] == 1)).astype(
        jnp.bfloat16
    )
    feature_width = tokens.shape[1]
    cold_send = (
        matmul(cold_pick, tokens).astype(jnp.bfloat16).reshape(experts, capacity, feature_width)
    )
    cold_recv = lax.all_to_all(
        cold_send, "expert", split_axis=0, concat_axis=0, tiled=True
    ).reshape(experts * capacity, feature_width)
    hot_input = hot_inputs(matmul(hot_pick, tokens).astype(jnp.bfloat16), hot_id, labels)
    cold_piece = lax.all_gather(cold_recv, "tensor", axis=1, tiled=True)
    hot_piece = lax.all_gather(hot_input, "tensor", axis=1, tiled=True)
    cold_gate = matmul(cold_piece, own_gate)
    cold_up = matmul(cold_piece, own_up)
    hot_gate = matmul(hot_piece, hot_gate_w)
    hot_up = matmul(hot_piece, hot_up_w)
    cold_part = matmul(swiglu(cold_gate, cold_up), own_down)
    hot_part = matmul(swiglu(hot_gate, hot_up), hot_down_w)
    model_width = cold_part.shape[1]
    came_back = lax.all_to_all(
        hot_part.reshape(experts, hot_rows, model_width),
        "expert",
        split_axis=0,
        concat_axis=0,
        tiled=True,
    )
    hot_part = lax.dynamic_index_in_dim(came_back, hot_id, 0, keepdims=False)
    returned = lax.all_to_all(
        cold_part.reshape(experts, capacity, model_width),
        "expert",
        split_axis=0,
        concat_axis=0,
        tiled=True,
    ).reshape(experts * capacity, model_width)
    assign_weight = route_share.reshape(2 * tok_rows) * is_live.astype(jnp.float32)
    cold_out = jnp.sum(
        (returned[target] * assign_weight[:, None]).reshape(tok_rows, 2, model_width), axis=1
    )
    hot_weight = jnp.sum(route_share * hot_match.astype(jnp.float32), axis=1)
    hot_out = hot_part[jnp.clip(hot_rank, 0, hot_rows - 1)] * hot_weight[:, None]
    mixed = lax.psum_scatter(cold_out + hot_out, "tensor", scatter_dimension=1, tiled=True).astype(
        jnp.bfloat16
    )
    expert_load = lax.psum(local_stats, "expert") / tok_rows
    return (mixed, expert_load)


def local(tokens, expert_ids, route_weight, gate_weight, up_weight, down_weight):
    experts = lax.axis_size("expert") * gate_weight.shape[0]
    width = lax.axis_size("tensor")
    width_ok = tokens.shape[1] >= 3 * LANES
    plain = width_ok and experts == lax.axis_size("expert") == 2 and width >= 16 and width & (width - 1) == 0
    if plain:
        return dense(tokens, expert_ids, route_weight, gate_weight, up_weight, down_weight)
    return general(tokens, expert_ids, route_weight, gate_weight, up_weight, down_weight)


def solution(mesh):
    placed = (
        P("expert", "tensor"),
        P("expert", None),
        P("expert", None),
        P("expert", None, "tensor"),
        P("expert", None, "tensor"),
        P("expert", "tensor", None),
    )
    return jax.shard_map(
        local, mesh=mesh, in_specs=placed, out_specs=(P("expert", "tensor"), P()), check_vma=False
    )
```

profile of v0, /device:TPU:0, one launch (start us, length us, event | category | flops | bytes accessed | tf_op | source)
XLA Modules:
  0.0 45.9 jit_solution(4558127359686215015)
XLA Ops:
  0.7 4.6 %collective-permute-start.1 = (bf16[48,384]{1,0:T(8,128)(2,1)}, bf16[48,384]{1,0:T(8,128)(2,1)S(1)}, u32[]{:S(2)}, u32[]{:S(2)}) collective-permute-start(bf16[48,384]{1,0:T(8,128)(2,1)} %refs_1_.1), channel_id=1, source_target_pairs={{0,13},{1,12},{2,15},{3,14},{4,9},{5,8},{6,11},{7,10},{8,5},{9,4},... | collective-permute-start | bytes 110600 | tf_op jit(solution)/shard_map/ppermute | solution.py:20
  5.3 0.0 collective-permute-start
  5.3 0.9 %collective-permute-start.9 = (bf16[48,384]{1,0:T(8,128)(2,1)}, bf16[48,384]{1,0:T(8,128)(2,1)S(1)}, u32[]{:S(2)}, u32[]{:S(2)}) collective-permute-start(bf16[48,384]{1,0:T(8,128)(2,1)} %refs_1_.1), channel_id=1, source_target_pairs={{0,5},{1,4},{2,7},{3,6},{4,1},{5,0},{6,3},{7,2},{8,13},{9,12},{10,... | collective-permute-start | bytes 110600 | tf_op jit(solution)/shard_map/ppermute | solution.py:20
  6.2 2.8 %collective-permute-done.9.refs_2_ = bf16[48,384]{1,0:T(8,128)(2,1)S(1)} collective-permute-done((bf16[48,384]{1,0:T(8,128)(2,1)}, bf16[48,384]{1,0:T(8,128)(2,1)S(1)}, u32[]{:S(2)}, u32[]{:S(2)}) %collective-permute-start.9) | collective-permute-done | bytes 36896 | tf_op jit(solution)/shard_map/ppermute | solution.py:20
  9.0 2.5 %collective-permute-start.15 = (bf16[2,48,384]{2,1,0:T(8,128)(2,1)S(1)}, bf16[2,48,384]{2,1,0:T(8,128)(2,1)S(1)}, u32[]{:S(2)}, u32[]{:S(2)}) collective-permute-start(bf16[2,48,384]{2,1,0:T(8,128)(2,1)S(1)} %shard_map.80.refs_0_), channel_id=1, source_target_pairs={{0,18},{1,19},{2,16},{3,17},{4,22},{5,23},{6,20},{7,21},{8,26},{9,... | collective-permute-start | bytes 221192 | tf_op jit(solution)/shard_map/ppermute | solution.py:20
  11.5 0.5 %collective-permute-start.13 = (bf16[2,48,384]{2,1,0:T(8,128)(2,1)S(1)}, bf16[2,48,384]{2,1,0:T(8,128)(2,1)S(1)}, u32[]{:S(2)}, u32[]{:S(2)}) collective-permute-start(bf16[2,48,384]{2,1,0:T(8,128)(2,1)S(1)} %shard_map.80.refs_0_), channel_id=1, source_target_pairs={{0,16},{1,17},{2,18},{3,19},{4,20},{5,21},{6,22},{7,23},{8,24},{9,... | collective-permute-start | bytes 221192 | tf_op jit(solution)/shard_map/ppermute | solution.py:20
  12.1 0.5 %collective-permute-start.11 = (bf16[2,48,384]{2,1,0:T(8,128)(2,1)S(1)}, bf16[2,48,384]{2,1,0:T(8,128)(2,1)S(1)}, u32[]{:S(2)}, u32[]{:S(2)}) collective-permute-start(bf16[2,48,384]{2,1,0:T(8,128)(2,1)S(1)} %shard_map.80.refs_0_), channel_id=1, source_target_pairs={{0,2},{1,3},{2,0},{3,1},{4,6},{5,7},{6,4},{7,5},{8,10},{9,11},{10,... | collective-permute-start | bytes 221192 | tf_op jit(solution)/shard_map/ppermute | solution.py:20
  12.6 0.0 collective-permute-done.1.refs_2_
  12.6 0.3 collective-permute-start.10
  12.8 0.0 collective-permute-done.refs_1_
  12.8 2.5 %collective-permute-start.7 = (bf16[2,48,384]{2,1,0:T(8,128)(2,1)S(1)}, bf16[2,48,384]{2,1,0:T(8,128)(2,1)S(1)}, u32[]{:S(2)}, u32[]{:S(2)}) collective-permute-start(bf16[2,48,384]{2,1,0:T(8,128)(2,1)S(1)} %shard_map.79.refs_0_), channel_id=1, source_target_pairs={{0,18},{1,19},{2,16},{3,17},{4,22},{5,23},{6,20},{7,21},{8,26},{9,... | collective-permute-start | bytes 221192 | tf_op jit(solution)/shard_map/ppermute | solution.py:20
  15.4 0.0 collective-permute-done.15.refs_6_
  15.4 1.1 %collective-permute-start.5 = (bf16[2,48,384]{2,1,0:T(8,128)(2,1)S(1)}, bf16[2,48,384]{2,1,0:T(8,128)(2,1)S(1)}, u32[]{:S(2)}, u32[]{:S(2)}) collective-permute-start(bf16[2,48,384]{2,1,0:T(8,128)(2,1)S(1)} %shard_map.79.refs_0_), channel_id=1, source_target_pairs={{0,16},{1,17},{2,18},{3,19},{4,20},{5,21},{6,22},{7,23},{8,24},{9,... | collective-permute-start | bytes 221192 | tf_op jit(solution)/shard_map/ppermute | solution.py:20
  16.5 0.2 collective-permute-done.13.refs_4_
  16.7 1.4 %collective-permute-start.3 = (bf16[2,48,384]{2,1,0:T(8,128)(2,1)S(1)}, bf16[2,48,384]{2,1,0:T(8,128)(2,1)S(1)}, u32[]{:S(2)}, u32[]{:S(2)}) collective-permute-start(bf16[2,48,384]{2,1,0:T(8,128)(2,1)S(1)} %shard_map.79.refs_0_), channel_id=1, source_target_pairs={{0,2},{1,3},{2,0},{3,1},{4,6},{5,7},{6,4},{7,5},{8,10},{9,11},{10,... | collective-permute-start | bytes 221192 | tf_op jit(solution)/shard_map/ppermute | solution.py:20
  18.1 0.0 collective-permute-done.11.refs_2_
  18.1 0.0 collective-permute-start.16
  18.1 0.0 collective-permute-done.10.refs_1_
  18.1 0.5 %collective-permute-start.14 = (bf16[2,48,384]{2,1,0:T(8,128)(2,1)S(1)}, bf16[2,48,384]{2,1,0:T(8,128)(2,1)S(1)}, u32[]{:S(2)}, u32[]{:S(2)}) collective-permute-start(bf16[2,48,384]{2,1,0:T(8,128)(2,1)S(1)} %collective-permute-done.13.refs_4_), channel_id=1, source_target_pairs={{0,1},{1,0},{2,3},{3,2},{4,5},{5,4},{6,7},{7,6},{8,9},{9,8},{10,11... | collective-permute-start | bytes 221192 | tf_op jit(solution)/shard_map/ppermute | solution.py:20
  18.6 0.0 collective-permute-done.7.refs_6_
  18.6 0.1 collective-permute-start.12
  18.7 1.2 %collective-permute-done.5.refs_4_ = bf16[2,48,384]{2,1,0:T(8,128)(2,1)S(1)} collective-permute-done((bf16[2,48,384]{2,1,0:T(8,128)(2,1)S(1)}, bf16[2,48,384]{2,1,0:T(8,128)(2,1)S(1)}, u32[]{:S(2)}, u32[]{:S(2)}) %collective-permute-start.5) | collective-permute-done | bytes 73760 | tf_op jit(solution)/shard_map/ppermute | solution.py:20
  19.9 0.0 collective-permute-start.2
  19.9 1.1 %collective-permute-done.3.refs_2_ = bf16[2,48,384]{2,1,0:T(8,128)(2,1)S(1)} collective-permute-done((bf16[2,48,384]{2,1,0:T(8,128)(2,1)S(1)}, bf16[2,48,384]{2,1,0:T(8,128)(2,1)S(1)}, u32[]{:S(2)}, u32[]{:S(2)}) %collective-permute-start.3) | collective-permute-done | bytes 73760 | tf_op jit(solution)/shard_map/ppermute | solution.py:20
  21.1 0.0 collective-permute-start.8
  21.1 0.0 collective-permute-done.16.refs_7_
  21.1 0.5 %collective-permute-start.6 = (bf16[2,48,384]{2,1,0:T(8,128)(2,1)S(1)}, bf16[2,48,384]{2,1,0:T(8,128)(2,1)S(1)}, u32[]{:S(2)}, u32[]{:S(2)}) collective-permute-start(bf16[2,48,384]{2,1,0:T(8,128)(2,1)S(1)} %collective-permute-done.5.refs_4_), channel_id=1, source_target_pairs={{0,1},{1,0},{2,3},{3,2},{4,5},{5,4},{6,7},{7,6},{8,9},{9,8},{10,11... | collective-permute-start | bytes 221192 | tf_op jit(solution)/shard_map/ppermute | solution.py:20
  21.6 0.0 collective-permute-done.14.refs_5_
  21.6 0.1 collective-permute-start.4
  21.6 0.0 collective-permute-done.12.refs_3_
  21.7 1.2 %shard_map.81 = (f32[96,512]{1,0:T(8,128)S(1)}, f32[96,512]{1,0:T(8,128)S(1)}) custom-call(bf16[2,48,384]{2,1,0:T(8,128)(2,1)S(1)} %shard_map.80.refs_0_, bf16[2,48,384]{2,1,0:T(8,128)(2,1)S(1)} %collective-permute-done.10.refs_1_, bf16[2,48,384]{2,1,0:T(8,128)(2,1)S(1)} %collective-permute-done.11.refs_2_, ...), custom_call_target="tpu_custom_call" | custom-call | flops 1207959552 | bytes 6291456 | tf_op jit(solution)/shard_map/pallas_call | solution.py:151
  22.8 0.0 collective-permute-done.2.refs_1_
  22.8 0.0 collective-permute-done.8.refs_7_
  22.8 0.0 collective-permute-done.6.refs_5_
  22.9 0.0 collective-permute-done.4.refs_3_
  22.9 1.2 %shard_map.82.hidden = bf16[96,512]{1,0:T(8,128)(2,1)S(1)} custom-call(bf16[2,48,384]{2,1,0:T(8,128)(2,1)S(1)} %shard_map.79.refs_0_, bf16[2,48,384]{2,1,0:T(8,128)(2,1)S(1)} %collective-permute-done.2.refs_1_, bf16[2,48,384]{2,1,0:T(8,128)(2,1)S(1)} %collective-permute-done.3.refs_2_, bf16[2,48,384]{2,1,0:T(8,128)(2,1)S(1)} %collective-permute-done.4.refs_3_, ...), custom_call_target="tpu_custom_call" | custom-call | flops 1207959552 | bytes 6291456 | tf_op jit(solution)/shard_map/pallas_call | solution.py:151
  24.0 0.0 copy-start.4
  24.0 0.0 copy-start.5
  24.1 0.7 %shard_map.86 = (bf16[2,2,2,48,384]{4,3,2,1,0:T(8,128)(2,1)S(1)}, f32[2,2,2,48,384]{4,3,2,1,0:T(8,128)S(1)}) custom-call(bf16[96,512]{1,0:T(8,128)(2,1)S(1)} %shard_map.82.hidden, bf16[1,512,6144]{2,1,0:T(8,128)(2,1)S(1)} %copy-done), custom_call_target="tpu_custom_call" | custom-call | flops 301989888 | bytes 3145728 | tf_op jit(solution)/shard_map/pallas_call | solution.py:151
  24.7 0.5 %collective-permute-start.21 = (bf16[2,2,2,48,384]{4,3,2,1,0:T(8,128)(2,1)S(1)}, bf16[2,2,2,48,384]{4,3,2,1,0:T(8,128)(2,1)S(1)}, u32[]{:S(2)}, u32[]{:S(2)}) collective-permute-start(bf16[2,2,2,48,384]{4,3,2,1,0:T(8,128)(2,1)S(1)} %get-tuple-element.35), channel_id=1, source_target_pairs={{0,1},{1,0},{2,3},{3,2},{4,5},{5,4},{6,7},{7,6},{8,9},{9,8},{10,11... | collective-permute-start | bytes 884744 | tf_op jit(solution)/shard_map/ppermute | solution.py:20
  25.3 0.7 %shard_map.83 = (bf16[2,2,2,48,384]{4,3,2,1,0:T(8,128)(2,1)S(1)}, f32[2,2,2,48,384]{4,3,2,1,0:T(8,128)S(1)}) custom-call(bf16[96,512]{1,0:T(8,128)(2,1)S(1)} %shard_map.82.hidden, bf16[1,512,6144]{2,1,0:T(8,128)(2,1)S(1)} %copy-done), custom_call_target="tpu_custom_call" | custom-call | flops 301989888 | bytes 3145728 | tf_op jit(solution)/shard_map/pallas_call | solution.py:151
  25.9 0.1 collective-permute-start.17
  26.1 0.4 collective-permute-done.21.arrived
  26.5 0.1 shard_map.87
  26.5 1.5 %collective-permute-start.22 = (bf16[96,384]{1,0:T(8,128)(2,1)S(1)}, bf16[96,384]{1,0:T(8,128)(2,1)S(1)}, u32[]{:S(2)}, u32[]{:S(2)}) collective-permute-start(bf16[96,384]{1,0:T(8,128)(2,1)S(1)} %get-tuple-element.37), channel_id=1, source_target_pairs={{0,16},{1,17},{2,18},{3,19},{4,20},{5,21},{6,22},{7,23},{8,24},{9,... | collective-permute-start | bytes 221192 | tf_op jit(solution)/shard_map/ppermute | solution.py:20
  28.1 0.1 shard_map.77
  28.2 0.1 shard_map.84
  28.3 0.9 %collective-permute-start.18 = (bf16[112,384]{1,0:T(8,128)(2,1)S(1)}, bf16[112,384]{1,0:T(8,128)(2,1)S(1)}, u32[]{:S(2)}, u32[]{:S(2)}) collective-permute-start(bf16[112,384]{1,0:T(8,128)(2,1)S(1)} %get-tuple-element.30), channel_id=1, source_target_pairs={{0,16},{1,17},{2,18},{3,19},{4,20},{5,21},{6,22},{7,23},{8,24},{9,... | collective-permute-start | bytes 258056 | tf_op jit(solution)/shard_map/ppermute | solution.py:20
  29.2 1.1 %collective-permute-start.23 = (bf16[2,48,384]{2,1,0:T(8,128)(2,1)S(1)}, bf16[2,48,384]{2,1,0:T(8,128)(2,1)S(1)}, u32[]{:S(2)}, u32[]{:S(2)}) collective-permute-start(bf16[2,48,384]{2,1,0:T(8,128)(2,1)S(1)} %get-tuple-element.38), channel_id=1, source_target_pairs={{0,2},{1,3},{2,0},{3,1},{4,6},{5,7},{6,4},{7,5},{8,10},{9,11},{10,... | collective-permute-start | bytes 221192 | tf_op jit(solution)/shard_map/ppermute | solution.py:20
  30.3 1.5 %collective-permute-start.24 = (bf16[2,48,384]{2,1,0:T(8,128)(2,1)S(1)}, bf16[2,48,384]{2,1,0:T(8,128)(2,1)S(1)}, u32[]{:S(2)}, u32[]{:S(2)}) collective-permute-start(bf16[2,48,384]{2,1,0:T(8,128)(2,1)S(1)} %get-tuple-element.39), channel_id=1, source_target_pairs={{0,18},{1,19},{2,16},{3,17},{4,22},{5,23},{6,20},{7,21},{8,26},{9,... | collective-permute-start | bytes 221192 | tf_op jit(solution)/shard_map/ppermute | solution.py:20
  31.8 0.8 %collective-permute-start.19 = (bf16[2,48,384]{2,1,0:T(8,128)(2,1)S(1)}, bf16[2,48,384]{2,1,0:T(8,128)(2,1)S(1)}, u32[]{:S(2)}, u32[]{:S(2)}) collective-permute-start(bf16[2,48,384]{2,1,0:T(8,128)(2,1)S(1)} %get-tuple-element.31), channel_id=1, source_target_pairs={{0,2},{1,3},{2,0},{3,1},{4,6},{5,7},{6,4},{7,5},{8,10},{9,11},{10,... | collective-permute-start | bytes 221192 | tf_op jit(solution)/shard_map/ppermute | solution.py:20
  32.6 1.5 %collective-permute-start.20 = (bf16[2,48,384]{2,1,0:T(8,128)(2,1)S(1)}, bf16[2,48,384]{2,1,0:T(8,128)(2,1)S(1)}, u32[]{:S(2)}, u32[]{:S(2)}) collective-permute-start(bf16[2,48,384]{2,1,0:T(8,128)(2,1)S(1)} %get-tuple-element.32), channel_id=1, source_target_pairs={{0,18},{1,19},{2,16},{3,17},{4,22},{5,23},{6,20},{7,21},{8,26},{9,... | collective-permute-start | bytes 221192 | tf_op jit(solution)/shard_map/ppermute | solution.py:20
  34.2 0.0 collective-permute-done.23.from_y
  34.2 1.8 %collective-permute-done.24.from_xy = bf16[2,48,384]{2,1,0:T(8,128)(2,1)S(1)} collective-permute-done((bf16[2,48,384]{2,1,0:T(8,128)(2,1)S(1)}, bf16[2,48,384]{2,1,0:T(8,128)(2,1)S(1)}, u32[]{:S(2)}, u32[]{:S(2)}) %collective-permute-start.24) | collective-permute-done | bytes 73760 | tf_op jit(solution)/shard_map/ppermute | solution.py:20
  36.0 0.1 shard_map.88
  36.1 0.6 %collective-permute-start.27 = (bf16[48,384]{1,0:T(8,128)(2,1)S(1)}, bf16[48,384]{1,0:T(8,128)(2,1)S(1)}, u32[]{:S(2)}, u32[]{:S(2)}) collective-permute-start(bf16[48,384]{1,0:T(8,128)(2,1)S(1)} %get-tuple-element.43), channel_id=1, source_target_pairs={{0,5},{1,4},{2,7},{3,6},{4,1},{5,0},{6,3},{7,2},{8,13},{9,12},{10,... | collective-permute-start | bytes 110600 | tf_op jit(solution)/shard_map/ppermute | solution.py:20
  36.6 1.7 %collective-permute-done.19.from_y = bf16[2,48,384]{2,1,0:T(8,128)(2,1)S(1)} collective-permute-done((bf16[2,48,384]{2,1,0:T(8,128)(2,1)S(1)}, bf16[2,48,384]{2,1,0:T(8,128)(2,1)S(1)}, u32[]{:S(2)}, u32[]{:S(2)}) %collective-permute-start.19) | collective-permute-done | bytes 73760 | tf_op jit(solution)/shard_map/ppermute | solution.py:20
  38.3 0.1 shard_map.85
  38.4 2.5 %collective-permute-start.25 = (bf16[48,384]{1,0:T(8,128)(2,1)S(1)}, bf16[48,384]{1,0:T(8,128)(2,1)S(1)}, u32[]{:S(2)}, u32[]{:S(2)}) collective-permute-start(bf16[48,384]{1,0:T(8,128)(2,1)S(1)} %get-tuple-element.41), channel_id=1, source_target_pairs={{0,13},{1,12},{2,15},{3,14},{4,9},{5,8},{6,11},{7,10},{8,5},{9,4},... | collective-permute-start | bytes 110600 | tf_op jit(solution)/shard_map/ppermute | solution.py:20
  40.9 0.8 %collective-permute-start.26 = (bf16[48,384]{1,0:T(8,128)(2,1)S(1)}, bf16[48,384]{1,0:T(8,128)(2,1)S(1)}, u32[]{:S(2)}, u32[]{:S(2)}) collective-permute-start(bf16[48,384]{1,0:T(8,128)(2,1)S(1)} %get-tuple-element.42), channel_id=1, source_target_pairs={{0,9},{1,8},{2,11},{3,10},{4,13},{5,12},{6,15},{7,14},{8,1},{9,0},... | collective-permute-start | bytes 110600 | tf_op jit(solution)/shard_map/ppermute | solution.py:20
  41.7 0.0 collective-permute-done.27.refs_2_
  41.7 2.1 %collective-permute-done.25.refs_0_ = bf16[48,384]{1,0:T(8,128)(2,1)S(1)} collective-permute-done((bf16[48,384]{1,0:T(8,128)(2,1)S(1)}, bf16[48,384]{1,0:T(8,128)(2,1)S(1)}, u32[]{:S(2)}, u32[]{:S(2)}) %collective-permute-start.25) | collective-permute-done | bytes 36896 | tf_op jit(solution)/shard_map/ppermute | solution.py:20
  43.8 1.5 %collective-permute-done.26.refs_1_ = bf16[48,384]{1,0:T(8,128)(2,1)S(1)} collective-permute-done((bf16[48,384]{1,0:T(8,128)(2,1)S(1)}, bf16[48,384]{1,0:T(8,128)(2,1)S(1)}, u32[]{:S(2)}, u32[]{:S(2)}) %collective-permute-start.26) | collective-permute-done | bytes 36896 | tf_op jit(solution)/shard_map/ppermute | solution.py:20
  45.3 0.6 %shard_map.89 = (bf16[48,384]{1,0:T(8,128)(2,1)}, f32[2,2]{1,0:T(2,128)}) custom-call(f32[16,128]{1,0:T(8,128)S(1)} %get-tuple-element.33.load, f32[48,384]{1,0:T(8,128)S(1)} %get-tuple-element.40.keep, bf16[48,384]{1,0:T(8,128)(2,1)S(1)} %collective-permute-done.25.refs_0_, bf16[48,384]{1,0:T(8,128)(2,1)S(1)} %collective-permute-done.26.refs_1_, ...), custom_call_target="tpu_custom_call" | custom-call | tf_op jit(solution)/shard_map/pallas_call | solution.py:151
  (17 shorter events, 0.0 us)
Async XLA Ops:
  0.6 8.4 %copy-start.3 = (bf16[48,384]{1,0:T(8,128)(2,1)S(1)}, bf16[48,384]{1,0:T(8,128)(2,1)}, u32[]{:S(2)}) copy-start(bf16[48,384]{1,0:T(8,128)(2,1)} %refs_1_.1) | copy-start | bytes 110596
  0.6 21.0 %copy-start = (bf16[1,512,6144]{2,1,0:T(8,128)(2,1)S(1)}, bf16[1,512,6144]{2,1,0:T(8,128)(2,1)}, u32[]{:S(2)}) copy-start(bf16[1,512,6144]{2,1,0:T(8,128)(2,1)} %weights.3) | copy-start | bytes 18874372
  0.7 21.0 %copy-start.2 = (bf16[1,6144,512]{2,1,0:T(8,128)(2,1)S(1)}, bf16[1,6144,512]{2,1,0:T(8,128)(2,1)}, u32[]{:S(2)}) copy-start(bf16[1,6144,512]{2,1,0:T(8,128)(2,1)} %refs_9_.3) | copy-start | bytes 18874372
  0.7 21.0 %copy-start.1 = (bf16[1,6144,512]{2,1,0:T(8,128)(2,1)S(1)}, bf16[1,6144,512]{2,1,0:T(8,128)(2,1)}, u32[]{:S(2)}) copy-start(bf16[1,6144,512]{2,1,0:T(8,128)(2,1)} %refs_8_.3) | copy-start | bytes 18874372
  0.7 11.9 %collective-permute-start.1 = (bf16[48,384]{1,0:T(8,128)(2,1)}, bf16[48,384]{1,0:T(8,128)(2,1)S(1)}, u32[]{:S(2)}, u32[]{:S(2)}) collective-permute-start(bf16[48,384]{1,0:T(8,128)(2,1)} %refs_1_.1), channel_id=1, source_target_pairs={{0,13},{1,12},{2,15},{3,14},{4,9},{5,8},{6,11},{7,10},{8,5},{9,4},... | collective-permute-start | bytes 110600 | tf_op jit(solution)/shard_map/ppermute | solution.py:20
  5.3 7.6 %collective-permute-start = (bf16[48,384]{1,0:T(8,128)(2,1)}, bf16[48,384]{1,0:T(8,128)(2,1)S(1)}, u32[]{:S(2)}, u32[]{:S(2)}) collective-permute-start(bf16[48,384]{1,0:T(8,128)(2,1)} %refs_1_.1), channel_id=1, source_target_pairs={{0,9},{1,8},{2,11},{3,10},{4,13},{5,12},{6,15},{7,14},{8,1},{9,0},... | collective-permute-start | bytes 110600 | tf_op jit(solution)/shard_map/ppermute | solution.py:20
  5.3 3.8 %collective-permute-start.9 = (bf16[48,384]{1,0:T(8,128)(2,1)}, bf16[48,384]{1,0:T(8,128)(2,1)S(1)}, u32[]{:S(2)}, u32[]{:S(2)}) collective-permute-start(bf16[48,384]{1,0:T(8,128)(2,1)} %refs_1_.1), channel_id=1, source_target_pairs={{0,5},{1,4},{2,7},{3,6},{4,1},{5,0},{6,3},{7,2},{8,13},{9,12},{10,... | collective-permute-start | bytes 110600 | tf_op jit(solution)/shard_map/ppermute | solution.py:20
  9.0 6.3 %collective-permute-start.15 = (bf16[2,48,384]{2,1,0:T(8,128)(2,1)S(1)}, bf16[2,48,384]{2,1,0:T(8,128)(2,1)S(1)}, u32[]{:S(2)}, u32[]{:S(2)}) collective-permute-start(bf16[2,48,384]{2,1,0:T(8,128)(2,1)S(1)} %shard_map.80.refs_0_), channel_id=1, source_target_pairs={{0,18},{1,19},{2,16},{3,17},{4,22},{5,23},{6,20},{7,21},{8,26},{9,... | collective-permute-start | bytes 221192 | tf_op jit(solution)/shard_map/ppermute | solution.py:20
  11.5 5.1 %collective-permute-start.13 = (bf16[2,48,384]{2,1,0:T(8,128)(2,1)S(1)}, bf16[2,48,384]{2,1,0:T(8,128)(2,1)S(1)}, u32[]{:S(2)}, u32[]{:S(2)}) collective-permute-start(bf16[2,48,384]{2,1,0:T(8,128)(2,1)S(1)} %shard_map.80.refs_0_), channel_id=1, source_target_pairs={{0,16},{1,17},{2,18},{3,19},{4,20},{5,21},{6,22},{7,23},{8,24},{9,... | collective-permute-start | bytes 221192 | tf_op jit(solution)/shard_map/ppermute | solution.py:20
  12.1 6.0 %collective-permute-start.11 = (bf16[2,48,384]{2,1,0:T(8,128)(2,1)S(1)}, bf16[2,48,384]{2,1,0:T(8,128)(2,1)S(1)}, u32[]{:S(2)}, u32[]{:S(2)}) collective-permute-start(bf16[2,48,384]{2,1,0:T(8,128)(2,1)S(1)} %shard_map.80.refs_0_), channel_id=1, source_target_pairs={{0,2},{1,3},{2,0},{3,1},{4,6},{5,7},{6,4},{7,5},{8,10},{9,11},{10,... | collective-permute-start | bytes 221192 | tf_op jit(solution)/shard_map/ppermute | solution.py:20
  12.6 5.5 %collective-permute-start.10 = (bf16[2,48,384]{2,1,0:T(8,128)(2,1)S(1)}, bf16[2,48,384]{2,1,0:T(8,128)(2,1)S(1)}, u32[]{:S(2)}, u32[]{:S(2)}) collective-permute-start(bf16[2,48,384]{2,1,0:T(8,128)(2,1)S(1)} %shard_map.80.refs_0_), channel_id=1, source_target_pairs={{0,1},{1,0},{2,3},{3,2},{4,5},{5,4},{6,7},{7,6},{8,9},{9,8},{10,11... | collective-permute-start | bytes 221192 | tf_op jit(solution)/shard_map/ppermute | solution.py:20
  12.8 5.8 %collective-permute-start.7 = (bf16[2,48,384]{2,1,0:T(8,128)(2,1)S(1)}, bf16[2,48,384]{2,1,0:T(8,128)(2,1)S(1)}, u32[]{:S(2)}, u32[]{:S(2)}) collective-permute-start(bf16[2,48,384]{2,1,0:T(8,128)(2,1)S(1)} %shard_map.79.refs_0_), channel_id=1, source_target_pairs={{0,18},{1,19},{2,16},{3,17},{4,22},{5,23},{6,20},{7,21},{8,26},{9,... | collective-permute-start | bytes 221192 | tf_op jit(solution)/shard_map/ppermute | solution.py:20
  15.4 4.6 %collective-permute-start.5 = (bf16[2,48,384]{2,1,0:T(8,128)(2,1)S(1)}, bf16[2,48,384]{2,1,0:T(8,128)(2,1)S(1)}, u32[]{:S(2)}, u32[]{:S(2)}) collective-permute-start(bf16[2,48,384]{2,1,0:T(8,128)(2,1)S(1)} %shard_map.79.refs_0_), channel_id=1, source_target_pairs={{0,16},{1,17},{2,18},{3,19},{4,20},{5,21},{6,22},{7,23},{8,24},{9,... | collective-permute-start | bytes 221192 | tf_op jit(solution)/shard_map/ppermute | solution.py:20
  16.7 4.4 %collective-permute-start.3 = (bf16[2,48,384]{2,1,0:T(8,128)(2,1)S(1)}, bf16[2,48,384]{2,1,0:T(8,128)(2,1)S(1)}, u32[]{:S(2)}, u32[]{:S(2)}) collective-permute-start(bf16[2,48,384]{2,1,0:T(8,128)(2,1)S(1)} %shard_map.79.refs_0_), channel_id=1, source_target_pairs={{0,2},{1,3},{2,0},{3,1},{4,6},{5,7},{6,4},{7,5},{8,10},{9,11},{10,... | collective-permute-start | bytes 221192 | tf_op jit(solution)/shard_map/ppermute | solution.py:20
  18.1 3.0 %collective-permute-start.16 = (bf16[2,48,384]{2,1,0:T(8,128)(2,1)S(1)}, bf16[2,48,384]{2,1,0:T(8,128)(2,1)S(1)}, u32[]{:S(2)}, u32[]{:S(2)}) collective-permute-start(bf16[2,48,384]{2,1,0:T(8,128)(2,1)S(1)} %collective-permute-done.15.refs_6_), channel_id=1, source_target_pairs={{0,1},{1,0},{2,3},{3,2},{4,5},{5,4},{6,7},{7,6},{8,9},{9,8},{10,11... | collective-permute-start | bytes 221192 | tf_op jit(solution)/shard_map/ppermute | solution.py:20
  18.1 3.5 %collective-permute-start.14 = (bf16[2,48,384]{2,1,0:T(8,128)(2,1)S(1)}, bf16[2,48,384]{2,1,0:T(8,128)(2,1)S(1)}, u32[]{:S(2)}, u32[]{:S(2)}) collective-permute-start(bf16[2,48,384]{2,1,0:T(8,128)(2,1)S(1)} %collective-permute-done.13.refs_4_), channel_id=1, source_target_pairs={{0,1},{1,0},{2,3},{3,2},{4,5},{5,4},{6,7},{7,6},{8,9},{9,8},{10,11... | collective-permute-start | bytes 221192 | tf_op jit(solution)/shard_map/ppermute | solution.py:20
  18.6 3.0 %collective-permute-start.12 = (bf16[2,48,384]{2,1,0:T(8,128)(2,1)S(1)}, bf16[2,48,384]{2,1,0:T(8,128)(2,1)S(1)}, u32[]{:S(2)}, u32[]{:S(2)}) collective-permute-start(bf16[2,48,384]{2,1,0:T(8,128)(2,1)S(1)} %collective-permute-done.11.refs_2_), channel_id=1, source_target_pairs={{0,1},{1,0},{2,3},{3,2},{4,5},{5,4},{6,7},{7,6},{8,9},{9,8},{10,11... | collective-permute-start | bytes 221192 | tf_op jit(solution)/shard_map/ppermute | solution.py:20
  19.9 2.9 %collective-permute-start.2 = (bf16[2,48,384]{2,1,0:T(8,128)(2,1)S(1)}, bf16[2,48,384]{2,1,0:T(8,128)(2,1)S(1)}, u32[]{:S(2)}, u32[]{:S(2)}) collective-permute-start(bf16[2,48,384]{2,1,0:T(8,128)(2,1)S(1)} %shard_map.79.refs_0_), channel_id=1, source_target_pairs={{0,1},{1,0},{2,3},{3,2},{4,5},{5,4},{6,7},{7,6},{8,9},{9,8},{10,11... | collective-permute-start | bytes 221192 | tf_op jit(solution)/shard_map/ppermute | solution.py:20
  21.1 1.8 %collective-permute-start.8 = (bf16[2,48,384]{2,1,0:T(8,128)(2,1)S(1)}, bf16[2,48,384]{2,1,0:T(8,128)(2,1)S(1)}, u32[]{:S(2)}, u32[]{:S(2)}) collective-permute-start(bf16[2,48,384]{2,1,0:T(8,128)(2,1)S(1)} %collective-permute-done.7.refs_6_), channel_id=1, source_target_pairs={{0,1},{1,0},{2,3},{3,2},{4,5},{5,4},{6,7},{7,6},{8,9},{9,8},{10,11... | collective-permute-start | bytes 221192 | tf_op jit(solution)/shard_map/ppermute | solution.py:20
  21.1 1.8 %collective-permute-start.6 = (bf16[2,48,384]{2,1,0:T(8,128)(2,1)S(1)}, bf16[2,48,384]{2,1,0:T(8,128)(2,1)S(1)}, u32[]{:S(2)}, u32[]{:S(2)}) collective-permute-start(bf16[2,48,384]{2,1,0:T(8,128)(2,1)S(1)} %collective-permute-done.5.refs_4_), channel_id=1, source_target_pairs={{0,1},{1,0},{2,3},{3,2},{4,5},{5,4},{6,7},{7,6},{8,9},{9,8},{10,11... | collective-permute-start | bytes 221192 | tf_op jit(solution)/shard_map/ppermute | solution.py:20
  21.6 1.3 %collective-permute-start.4 = (bf16[2,48,384]{2,1,0:T(8,128)(2,1)S(1)}, bf16[2,48,384]{2,1,0:T(8,128)(2,1)S(1)}, u32[]{:S(2)}, u32[]{:S(2)}) collective-permute-start(bf16[2,48,384]{2,1,0:T(8,128)(2,1)S(1)} %collective-permute-done.3.refs_2_), channel_id=1, source_target_pairs={{0,1},{1,0},{2,3},{3,2},{4,5},{5,4},{6,7},{7,6},{8,9},{9,8},{10,11... | collective-permute-start | bytes 221192 | tf_op jit(solution)/shard_map/ppermute | solution.py:20
  24.0 4.1 %copy-start.4 = (s32[48,2]{0,1:T(2,128)S(1)}, s32[48,2]{0,1:T(2,128)}, u32[]{:S(2)}) copy-start(s32[48,2]{0,1:T(2,128)} %param.7) | copy-start | bytes 1156
  24.0 4.0 %copy-start.5 = (s32[48,2]{0,1:T(2,128)S(1)}, s32[48,2]{0,1:T(2,128)}, u32[]{:S(2)}) copy-start(s32[48,2]{0,1:T(2,128)} %param.8) | copy-start | bytes 1156
  24.7 1.7 %collective-permute-start.21 = (bf16[2,2,2,48,384]{4,3,2,1,0:T(8,128)(2,1)S(1)}, bf16[2,2,2,48,384]{4,3,2,1,0:T(8,128)(2,1)S(1)}, u32[]{:S(2)}, u32[]{:S(2)}) collective-permute-start(bf16[2,2,2,48,384]{4,3,2,1,0:T(8,128)(2,1)S(1)} %get-tuple-element.35), channel_id=1, source_target_pairs={{0,1},{1,0},{2,3},{3,2},{4,5},{5,4},{6,7},{7,6},{8,9},{9,8},{10,11... | collective-permute-start | bytes 884744 | tf_op jit(solution)/shard_map/ppermute | solution.py:20
  25.9 2.3 %collective-permute-start.17 = (bf16[2,2,2,48,384]{4,3,2,1,0:T(8,128)(2,1)S(1)}, bf16[2,2,2,48,384]{4,3,2,1,0:T(8,128)(2,1)S(1)}, u32[]{:S(2)}, u32[]{:S(2)}) collective-permute-start(bf16[2,2,2,48,384]{4,3,2,1,0:T(8,128)(2,1)S(1)} %get-tuple-element.27), channel_id=1, source_target_pairs={{0,1},{1,0},{2,3},{3,2},{4,5},{5,4},{6,7},{7,6},{8,9},{9,8},{10,11... | collective-permute-start | bytes 884744 | tf_op jit(solution)/shard_map/ppermute | solution.py:20
  26.5 6.1 %collective-permute-start.22 = (bf16[96,384]{1,0:T(8,128)(2,1)S(1)}, bf16[96,384]{1,0:T(8,128)(2,1)S(1)}, u32[]{:S(2)}, u32[]{:S(2)}) collective-permute-start(bf16[96,384]{1,0:T(8,128)(2,1)S(1)} %get-tuple-element.37), channel_id=1, source_target_pairs={{0,16},{1,17},{2,18},{3,19},{4,20},{5,21},{6,22},{7,23},{8,24},{9,... | collective-permute-start | bytes 221192 | tf_op jit(solution)/shard_map/ppermute | solution.py:20
  28.3 10.0 %collective-permute-start.18 = (bf16[112,384]{1,0:T(8,128)(2,1)S(1)}, bf16[112,384]{1,0:T(8,128)(2,1)S(1)}, u32[]{:S(2)}, u32[]{:S(2)}) collective-permute-start(bf16[112,384]{1,0:T(8,128)(2,1)S(1)} %get-tuple-element.30), channel_id=1, source_target_pairs={{0,16},{1,17},{2,18},{3,19},{4,20},{5,21},{6,22},{7,23},{8,24},{9,... | collective-permute-start | bytes 258056 | tf_op jit(solution)/shard_map/ppermute | solution.py:20
  29.2 5.0 %collective-permute-start.23 = (bf16[2,48,384]{2,1,0:T(8,128)(2,1)S(1)}, bf16[2,48,384]{2,1,0:T(8,128)(2,1)S(1)}, u32[]{:S(2)}, u32[]{:S(2)}) collective-permute-start(bf16[2,48,384]{2,1,0:T(8,128)(2,1)S(1)} %get-tuple-element.38), channel_id=1, source_target_pairs={{0,2},{1,3},{2,0},{3,1},{4,6},{5,7},{6,4},{7,5},{8,10},{9,11},{10,... | collective-permute-start | bytes 221192 | tf_op jit(solution)/shard_map/ppermute | solution.py:20
  30.3 5.7 %collective-permute-start.24 = (bf16[2,48,384]{2,1,0:T(8,128)(2,1)S(1)}, bf16[2,48,384]{2,1,0:T(8,128)(2,1)S(1)}, u32[]{:S(2)}, u32[]{:S(2)}) collective-permute-start(bf16[2,48,384]{2,1,0:T(8,128)(2,1)S(1)} %get-tuple-element.39), channel_id=1, source_target_pairs={{0,18},{1,19},{2,16},{3,17},{4,22},{5,23},{6,20},{7,21},{8,26},{9,... | collective-permute-start | bytes 221192 | tf_op jit(solution)/shard_map/ppermute | solution.py:20
  31.8 6.5 %collective-permute-start.19 = (bf16[2,48,384]{2,1,0:T(8,128)(2,1)S(1)}, bf16[2,48,384]{2,1,0:T(8,128)(2,1)S(1)}, u32[]{:S(2)}, u32[]{:S(2)}) collective-permute-start(bf16[2,48,384]{2,1,0:T(8,128)(2,1)S(1)} %get-tuple-element.31), channel_id=1, source_target_pairs={{0,2},{1,3},{2,0},{3,1},{4,6},{5,7},{6,4},{7,5},{8,10},{9,11},{10,... | collective-permute-start | bytes 221192 | tf_op jit(solution)/shard_map/ppermute | solution.py:20
  32.6 5.7 %collective-permute-start.20 = (bf16[2,48,384]{2,1,0:T(8,128)(2,1)S(1)}, bf16[2,48,384]{2,1,0:T(8,128)(2,1)S(1)}, u32[]{:S(2)}, u32[]{:S(2)}) collective-permute-start(bf16[2,48,384]{2,1,0:T(8,128)(2,1)S(1)} %get-tuple-element.32), channel_id=1, source_target_pairs={{0,18},{1,19},{2,16},{3,17},{4,22},{5,23},{6,20},{7,21},{8,26},{9,... | collective-permute-start | bytes 221192 | tf_op jit(solution)/shard_map/ppermute | solution.py:20
  36.1 5.6 %collective-permute-start.27 = (bf16[48,384]{1,0:T(8,128)(2,1)S(1)}, bf16[48,384]{1,0:T(8,128)(2,1)S(1)}, u32[]{:S(2)}, u32[]{:S(2)}) collective-permute-start(bf16[48,384]{1,0:T(8,128)(2,1)S(1)} %get-tuple-element.43), channel_id=1, source_target_pairs={{0,5},{1,4},{2,7},{3,6},{4,1},{5,0},{6,3},{7,2},{8,13},{9,12},{10,... | collective-permute-start | bytes 110600 | tf_op jit(solution)/shard_map/ppermute | solution.py:20
  38.4 5.3 %collective-permute-start.25 = (bf16[48,384]{1,0:T(8,128)(2,1)S(1)}, bf16[48,384]{1,0:T(8,128)(2,1)S(1)}, u32[]{:S(2)}, u32[]{:S(2)}) collective-permute-start(bf16[48,384]{1,0:T(8,128)(2,1)S(1)} %get-tuple-element.41), channel_id=1, source_target_pairs={{0,13},{1,12},{2,15},{3,14},{4,9},{5,8},{6,11},{7,10},{8,5},{9,4},... | collective-permute-start | bytes 110600 | tf_op jit(solution)/shard_map/ppermute | solution.py:20
  40.9 4.4 %collective-permute-start.26 = (bf16[48,384]{1,0:T(8,128)(2,1)S(1)}, bf16[48,384]{1,0:T(8,128)(2,1)S(1)}, u32[]{:S(2)}, u32[]{:S(2)}) collective-permute-start(bf16[48,384]{1,0:T(8,128)(2,1)S(1)} %get-tuple-element.42), channel_id=1, source_target_pairs={{0,9},{1,8},{2,11},{3,10},{4,13},{5,12},{6,15},{7,14},{8,1},{9,0},... | collective-permute-start | bytes 110600 | tf_op jit(solution)/shard_map/ppermute | solution.py:20
where the time goes:
time: 46.5 us; the launch traced here: 45.9 us
  starting transfers between devices  27.4 us (59%)
  waiting for transfers between devices  12.9 us (28%)
  Pallas kernels  4.79 us (10%)
  between operations  0.79 us (2%)
    ppermute x28, starting transfers between devices, swap(): return lax.ppermute(value, AXES, pairs)  27.4 us
    ppermute x28, waiting for transfers between devices, swap(): return lax.ppermute(value, AXES, pairs)  12.9 us
    pallas_call x13, Pallas kernels, call(): pl.pallas_call(kernel, out_shape=outs, in_specs=[VMEM] * len(inputs), out...  4.79 us
  transfers between devices with their start and end apart: 28, of which 9 were waited for; matrix products, arithmetic and copies ran while one was open for 0% of the time, Pallas kernels for 5%

commit v1 on v0

--- a/solution.py
+++ b/solution.py
@@ -105,6 +105,12 @@
                 send[flip, group, slot] = sent[part].astype(send.dtype)
 
 
+def project_down_kernel(zs, *refs):
+    inputs, down_w, (hidden, send, keep, rows) = refs[:12], refs[12], refs[13:]
+    project_kernel(zs, True, *inputs, hidden, rows)
+    down_kernel(zs, hidden, down_w, send, keep)
+
+
 def add_kernel(keep, arrived, *refs):
     *stats, own, to_x, to_y, to_xy = refs
     slots, rows = own.shape[:2]
@@ -193,10 +199,11 @@
         scratch=[pltpu.VMEM((2 * rows, len(sets[0]) * model // pieces_z), bf16)],
         estimate=estimate,
     )
-    hidden = call(
-        functools.partial(project_kernel, sets[1], True),
-        shape((2 * rows, units), bf16),
-        (*both[1], *weights, *first),
+    far_block = (2, 2, len(sets[1]), rows, width)
+    hidden, *far_parts = call(
+        functools.partial(project_down_kernel, sets[1]),
+        (shape((2 * rows, units), bf16), shape(far_block, bf16), shape(far_block, f32)),
+        (*both[1], *weights, *first, down_weight),
         scratch=[pltpu.VMEM((2 * rows, len(sets[1]) * model // pieces_z), bf16)],
         estimate=estimate,
     )
@@ -207,12 +214,15 @@
     for name, zs in (("far", sets[1]), ("near", sets[0])):
         block = (len(zs), rows, width)
         extra = [stats] if name == "far" else []
-        send, keep = call(
-            functools.partial(down_kernel, zs),
-            (shape((2, 2, *block), bf16), shape((2, 2, *block), f32)),
-            (hidden, down_weight),
-            estimate=cost(2 * rows * model * units, model * units),
-        )
+        if name == "far":
+            send, keep = far_parts
+        else:
+            send, keep = call(
+                functools.partial(down_kernel, zs),
+                (shape((2, 2, *block), bf16), shape((2, 2, *block), f32)),
+                (hidden, down_weight),
+                estimate=cost(2 * rows * model * units, model * units),
+            )
         arrived = swap(send, 0, 1)
         own, to_x, to_y, to_xy = call(
             add_kernel,

time: 46.5 us -> 47.2 us (1.015)
  waiting for transfers between devices: 12.9 us -> 14.2 us
    ppermute x28, waiting for transfers between devices: 12.9 us -> 14.2 us  [swap(): return lax.ppermute(value, AXES, pairs)]
    pallas_call x13 -> x12, Pallas kernels: 4.79 us -> 4.76 us  [call(): pl.pallas_call(kernel, out_shape=outs, in_specs=[VMEM] * len(inputs), out...]
  transfers between devices with their start and end apart: 28 -> 28, of which waited for: 9 -> 10; matrix products, arithmetic and copies ran while one was open for 0% -> 0% of each run, Pallas kernels for 5% -> 3%
where the time goes in v1:
time: 47.2 us; the launch traced here: 46.8 us
  starting transfers between devices  27 us (57%)
  waiting for transfers between devices  14.2 us (30%)
  Pallas kernels  4.76 us (10%)
  between operations  0.79 us (2%)
    ppermute x28, starting transfers between devices, swap(): return lax.ppermute(value, AXES, pairs)  27 us
    ppermute x28, waiting for transfers between devices, swap(): return lax.ppermute(value, AXES, pairs)  14.2 us
    pallas_call x12, Pallas kernels, call(): pl.pallas_call(kernel, out_shape=outs, in_specs=[VMEM] * len(inputs), out...  4.76 us
  transfers between devices with their start and end apart: 28, of which 10 were waited for; matrix products, arithmetic and copies ran while one was open for 0% of the time, Pallas kernels for 3%

profile of v1, /device:TPU:0, one launch (start us, length us, event | category | flops | bytes accessed | tf_op | source)
XLA Modules:
  0.0 46.8 jit_solution(18335184268728915974)
XLA Ops:
  0.7 4.6 %collective-permute-start.1 = (bf16[48,384]{1,0:T(8,128)(2,1)}, bf16[48,384]{1,0:T(8,128)(2,1)S(1)}, u32[]{:S(2)}, u32[]{:S(2)}) collective-permute-start(bf16[48,384]{1,0:T(8,128)(2,1)} %refs_1_.1), channel_id=1, source_target_pairs={{0,13},{1,12},{2,15},{3,14},{4,9},{5,8},{6,11},{7,10},{8,5},{9,4},... | collective-permute-start | bytes 110600 | tf_op jit(solution)/shard_map/ppermute | solution.py:20
  5.3 0.0 collective-permute-start
  5.3 0.9 %collective-permute-start.9 = (bf16[48,384]{1,0:T(8,128)(2,1)}, bf16[48,384]{1,0:T(8,128)(2,1)S(1)}, u32[]{:S(2)}, u32[]{:S(2)}) collective-permute-start(bf16[48,384]{1,0:T(8,128)(2,1)} %refs_1_.1), channel_id=1, source_target_pairs={{0,5},{1,4},{2,7},{3,6},{4,1},{5,0},{6,3},{7,2},{8,13},{9,12},{10,... | collective-permute-start | bytes 110600 | tf_op jit(solution)/shard_map/ppermute | solution.py:20
  6.2 2.8 %collective-permute-done.9.refs_2_ = bf16[48,384]{1,0:T(8,128)(2,1)S(1)} collective-permute-done((bf16[48,384]{1,0:T(8,128)(2,1)}, bf16[48,384]{1,0:T(8,128)(2,1)S(1)}, u32[]{:S(2)}, u32[]{:S(2)}) %collective-permute-start.9) | collective-permute-done | bytes 36896 | tf_op jit(solution)/shard_map/ppermute | solution.py:20
  9.0 2.5 %collective-permute-start.15 = (bf16[2,48,384]{2,1,0:T(8,128)(2,1)S(1)}, bf16[2,48,384]{2,1,0:T(8,128)(2,1)S(1)}, u32[]{:S(2)}, u32[]{:S(2)}) collective-permute-start(bf16[2,48,384]{2,1,0:T(8,128)(2,1)S(1)} %shard_map.80.refs_0_), channel_id=1, source_target_pairs={{0,18},{1,19},{2,16},{3,17},{4,22},{5,23},{6,20},{7,21},{8,26},{9,... | collective-permute-start | bytes 221192 | tf_op jit(solution)/shard_map/ppermute | solution.py:20
  11.5 0.5 %collective-permute-start.13 = (bf16[2,48,384]{2,1,0:T(8,128)(2,1)S(1)}, bf16[2,48,384]{2,1,0:T(8,128)(2,1)S(1)}, u32[]{:S(2)}, u32[]{:S(2)}) collective-permute-start(bf16[2,48,384]{2,1,0:T(8,128)(2,1)S(1)} %shard_map.80.refs_0_), channel_id=1, source_target_pairs={{0,16},{1,17},{2,18},{3,19},{4,20},{5,21},{6,22},{7,23},{8,24},{9,... | collective-permute-start | bytes 221192 | tf_op jit(solution)/shard_map/ppermute | solution.py:20
  12.1 0.5 %collective-permute-start.11 = (bf16[2,48,384]{2,1,0:T(8,128)(2,1)S(1)}, bf16[2,48,384]{2,1,0:T(8,128)(2,1)S(1)}, u32[]{:S(2)}, u32[]{:S(2)}) collective-permute-start(bf16[2,48,384]{2,1,0:T(8,128)(2,1)S(1)} %shard_map.80.refs_0_), channel_id=1, source_target_pairs={{0,2},{1,3},{2,0},{3,1},{4,6},{5,7},{6,4},{7,5},{8,10},{9,11},{10,... | collective-permute-start | bytes 221192 | tf_op jit(solution)/shard_map/ppermute | solution.py:20
  12.6 0.0 collective-permute-done.1.refs_2_
  12.6 0.3 collective-permute-start.10
  12.8 0.0 collective-permute-done.refs_1_
  12.8 2.5 %collective-permute-start.7 = (bf16[2,48,384]{2,1,0:T(8,128)(2,1)S(1)}, bf16[2,48,384]{2,1,0:T(8,128)(2,1)S(1)}, u32[]{:S(2)}, u32[]{:S(2)}) collective-permute-start(bf16[2,48,384]{2,1,0:T(8,128)(2,1)S(1)} %shard_map.79.refs_0_), channel_id=1, source_target_pairs={{0,18},{1,19},{2,16},{3,17},{4,22},{5,23},{6,20},{7,21},{8,26},{9,... | collective-permute-start | bytes 221192 | tf_op jit(solution)/shard_map/ppermute | solution.py:20
  15.4 0.0 collective-permute-done.15.refs_6_
  15.4 1.1 %collective-permute-start.5 = (bf16[2,48,384]{2,1,0:T(8,128)(2,1)S(1)}, bf16[2,48,384]{2,1,0:T(8,128)(2,1)S(1)}, u32[]{:S(2)}, u32[]{:S(2)}) collective-permute-start(bf16[2,48,384]{2,1,0:T(8,128)(2,1)S(1)} %shard_map.79.refs_0_), channel_id=1, source_target_pairs={{0,16},{1,17},{2,18},{3,19},{4,20},{5,21},{6,22},{7,23},{8,24},{9,... | collective-permute-start | bytes 221192 | tf_op jit(solution)/shard_map/ppermute | solution.py:20
  16.5 0.2 collective-permute-done.13.refs_4_
  16.7 1.4 %collective-permute-start.3 = (bf16[2,48,384]{2,1,0:T(8,128)(2,1)S(1)}, bf16[2,48,384]{2,1,0:T(8,128)(2,1)S(1)}, u32[]{:S(2)}, u32[]{:S(2)}) collective-permute-start(bf16[2,48,384]{2,1,0:T(8,128)(2,1)S(1)} %shard_map.79.refs_0_), channel_id=1, source_target_pairs={{0,2},{1,3},{2,0},{3,1},{4,6},{5,7},{6,4},{7,5},{8,10},{9,11},{10,... | collective-permute-start | bytes 221192 | tf_op jit(solution)/shard_map/ppermute | solution.py:20
  18.1 0.0 collective-permute-done.11.refs_2_
  18.1 0.0 collective-permute-start.16
  18.1 0.0 collective-permute-done.10.refs_1_
  18.1 0.5 %collective-permute-start.14 = (bf16[2,48,384]{2,1,0:T(8,128)(2,1)S(1)}, bf16[2,48,384]{2,1,0:T(8,128)(2,1)S(1)}, u32[]{:S(2)}, u32[]{:S(2)}) collective-permute-start(bf16[2,48,384]{2,1,0:T(8,128)(2,1)S(1)} %collective-permute-done.13.refs_4_), channel_id=1, source_target_pairs={{0,1},{1,0},{2,3},{3,2},{4,5},{5,4},{6,7},{7,6},{8,9},{9,8},{10,11... | collective-permute-start | bytes 221192 | tf_op jit(solution)/shard_map/ppermute | solution.py:20
  18.6 0.0 collective-permute-done.7.refs_6_
  18.6 0.1 collective-permute-start.12
  18.7 1.2 %collective-permute-done.5.refs_4_ = bf16[2,48,384]{2,1,0:T(8,128)(2,1)S(1)} collective-permute-done((bf16[2,48,384]{2,1,0:T(8,128)(2,1)S(1)}, bf16[2,48,384]{2,1,0:T(8,128)(2,1)S(1)}, u32[]{:S(2)}, u32[]{:S(2)}) %collective-permute-start.5) | collective-permute-done | bytes 73760 | tf_op jit(solution)/shard_map/ppermute | solution.py:20
  19.9 0.0 collective-permute-start.2
  19.9 1.1 %collective-permute-done.3.refs_2_ = bf16[2,48,384]{2,1,0:T(8,128)(2,1)S(1)} collective-permute-done((bf16[2,48,384]{2,1,0:T(8,128)(2,1)S(1)}, bf16[2,48,384]{2,1,0:T(8,128)(2,1)S(1)}, u32[]{:S(2)}, u32[]{:S(2)}) %collective-permute-start.3) | collective-permute-done | bytes 73760 | tf_op jit(solution)/shard_map/ppermute | solution.py:20
  21.1 0.0 collective-permute-start.8
  21.1 0.0 collective-permute-done.16.refs_7_
  21.1 0.5 %collective-permute-start.6 = (bf16[2,48,384]{2,1,0:T(8,128)(2,1)S(1)}, bf16[2,48,384]{2,1,0:T(8,128)(2,1)S(1)}, u32[]{:S(2)}, u32[]{:S(2)}) collective-permute-start(bf16[2,48,384]{2,1,0:T(8,128)(2,1)S(1)} %collective-permute-done.5.refs_4_), channel_id=1, source_target_pairs={{0,1},{1,0},{2,3},{3,2},{4,5},{5,4},{6,7},{7,6},{8,9},{9,8},{10,11... | collective-permute-start | bytes 221192 | tf_op jit(solution)/shard_map/ppermute | solution.py:20
  21.6 0.0 collective-permute-done.14.refs_5_
  21.6 0.1 collective-permute-start.4
  21.6 0.0 collective-permute-done.12.refs_3_
  21.7 1.2 %shard_map.81 = (f32[96,512]{1,0:T(8,128)S(1)}, f32[96,512]{1,0:T(8,128)S(1)}) custom-call(bf16[2,48,384]{2,1,0:T(8,128)(2,1)S(1)} %shard_map.80.refs_0_, bf16[2,48,384]{2,1,0:T(8,128)(2,1)S(1)} %collective-permute-done.10.refs_1_, bf16[2,48,384]{2,1,0:T(8,128)(2,1)S(1)} %collective-permute-done.11.refs_2_, ...), custom_call_target="tpu_custom_call" | custom-call | flops 1207959552 | bytes 6291456 | tf_op jit(solution)/shard_map/pallas_call | solution.py:157
  22.8 0.0 collective-permute-done.2.refs_1_
  22.8 0.0 collective-permute-done.8.refs_7_
  22.9 0.0 collective-permute-done.6.refs_5_
  22.9 1.8 %shard_map.82 = (bf16[96,512]{1,0:T(8,128)(2,1)S(1)}, bf16[2,2,2,48,384]{4,3,2,1,0:T(8,128)(2,1)S(1)}, f32[2,2,2,48,384]{4,3,2,1,0:T(8,128)S(1)}) custom-call(bf16[2,48,384]{2,1,0:T(8,128)(2,1)S(1)} %shard_map.79.refs_0_, bf16[2,48,384]{2,1,0:T(8,128)(2,1)S(1)} %collective-permute-done.2.refs_1_, bf16[2,48,384]{2,1,0:T(8,128)(2,1)S(1)} %collective-permute-done.3.refs_2_, ...), custom_call_target="tpu_custom_call" | custom-call | flops 1207959552 | bytes 6291456 | tf_op jit(solution)/shard_map/pallas_call | solution.py:157
  24.7 0.0 copy-start.4
  24.7 0.0 copy-start.5
  24.7 0.7 %shard_map.85 = (bf16[2,2,2,48,384]{4,3,2,1,0:T(8,128)(2,1)S(1)}, f32[2,2,2,48,384]{4,3,2,1,0:T(8,128)S(1)}) custom-call(bf16[96,512]{1,0:T(8,128)(2,1)S(1)} %get-tuple-element.35.hidden, bf16[1,512,6144]{2,1,0:T(8,128)(2,1)S(1)} %copy-done), custom_call_target="tpu_custom_call" | custom-call | flops 301989888 | bytes 3145728 | tf_op jit(solution)/shard_map/pallas_call | solution.py:157
  25.4 0.5 %collective-permute-start.21 = (bf16[2,2,2,48,384]{4,3,2,1,0:T(8,128)(2,1)S(1)}, bf16[2,2,2,48,384]{4,3,2,1,0:T(8,128)(2,1)S(1)}, u32[]{:S(2)}, u32[]{:S(2)}) collective-permute-start(bf16[2,2,2,48,384]{4,3,2,1,0:T(8,128)(2,1)S(1)} %get-tuple-element.37), channel_id=1, source_target_pairs={{0,1},{1,0},{2,3},{3,2},{4,5},{5,4},{6,7},{7,6},{8,9},{9,8},{10,11... | collective-permute-start | bytes 884744 | tf_op jit(solution)/shard_map/ppermute | solution.py:20
  25.9 0.1 collective-permute-start.17
  26.0 1.1 %collective-permute-done.21.arrived = bf16[2,2,2,48,384]{4,3,2,1,0:T(8,128)(2,1)S(1)} collective-permute-done((bf16[2,2,2,48,384]{4,3,2,1,0:T(8,128)(2,1)S(1)}, bf16[2,2,2,48,384]{4,3,2,1,0:T(8,128)(2,1)S(1)}, u32[]{:S(2)}, u32[]{:S(2)}) %collective-permute-start.21) | collective-permute-done | bytes 294944 | tf_op jit(solution)/shard_map/ppermute | solution.py:20
  27.1 0.1 shard_map.86
  27.2 1.6 %collective-permute-start.22 = (bf16[96,384]{1,0:T(8,128)(2,1)S(1)}, bf16[96,384]{1,0:T(8,128)(2,1)S(1)}, u32[]{:S(2)}, u32[]{:S(2)}) collective-permute-start(bf16[96,384]{1,0:T(8,128)(2,1)S(1)} %get-tuple-element.39), channel_id=1, source_target_pairs={{0,16},{1,17},{2,18},{3,19},{4,20},{5,21},{6,22},{7,23},{8,24},{9,... | collective-permute-start | bytes 221192 | tf_op jit(solution)/shard_map/ppermute | solution.py:20
  28.7 0.1 shard_map.77
  28.8 0.0 collective-permute-done.17.arrived
  28.9 0.1 shard_map.83
  28.9 0.6 %collective-permute-start.18 = (bf16[112,384]{1,0:T(8,128)(2,1)S(1)}, bf16[112,384]{1,0:T(8,128)(2,1)S(1)}, u32[]{:S(2)}, u32[]{:S(2)}) collective-permute-start(bf16[112,384]{1,0:T(8,128)(2,1)S(1)} %get-tuple-element.31), channel_id=1, source_target_pairs={{0,16},{1,17},{2,18},{3,19},{4,20},{5,21},{6,22},{7,23},{8,24},{9,... | collective-permute-start | bytes 258056 | tf_op jit(solution)/shard_map/ppermute | solution.py:20
  29.5 1.4 %collective-permute-start.23 = (bf16[2,48,384]{2,1,0:T(8,128)(2,1)S(1)}, bf16[2,48,384]{2,1,0:T(8,128)(2,1)S(1)}, u32[]{:S(2)}, u32[]{:S(2)}) collective-permute-start(bf16[2,48,384]{2,1,0:T(8,128)(2,1)S(1)} %get-tuple-element.40), channel_id=1, source_target_pairs={{0,2},{1,3},{2,0},{3,1},{4,6},{5,7},{6,4},{7,5},{8,10},{9,11},{10,... | collective-permute-start | bytes 221192 | tf_op jit(solution)/shard_map/ppermute | solution.py:20
  30.9 1.5 %collective-permute-start.24 = (bf16[2,48,384]{2,1,0:T(8,128)(2,1)S(1)}, bf16[2,48,384]{2,1,0:T(8,128)(2,1)S(1)}, u32[]{:S(2)}, u32[]{:S(2)}) collective-permute-start(bf16[2,48,384]{2,1,0:T(8,128)(2,1)S(1)} %get-tuple-element.41), channel_id=1, source_target_pairs={{0,18},{1,19},{2,16},{3,17},{4,22},{5,23},{6,20},{7,21},{8,26},{9,... | collective-permute-start | bytes 221192 | tf_op jit(solution)/shard_map/ppermute | solution.py:20
  32.5 0.7 %collective-permute-start.19 = (bf16[2,48,384]{2,1,0:T(8,128)(2,1)S(1)}, bf16[2,48,384]{2,1,0:T(8,128)(2,1)S(1)}, u32[]{:S(2)}, u32[]{:S(2)}) collective-permute-start(bf16[2,48,384]{2,1,0:T(8,128)(2,1)S(1)} %get-tuple-element.32), channel_id=1, source_target_pairs={{0,2},{1,3},{2,0},{3,1},{4,6},{5,7},{6,4},{7,5},{8,10},{9,11},{10,... | collective-permute-start | bytes 221192 | tf_op jit(solution)/shard_map/ppermute | solution.py:20
  33.2 1.2 %collective-permute-start.20 = (bf16[2,48,384]{2,1,0:T(8,128)(2,1)S(1)}, bf16[2,48,384]{2,1,0:T(8,128)(2,1)S(1)}, u32[]{:S(2)}, u32[]{:S(2)}) collective-permute-start(bf16[2,48,384]{2,1,0:T(8,128)(2,1)S(1)} %get-tuple-element.33), channel_id=1, source_target_pairs={{0,18},{1,19},{2,16},{3,17},{4,22},{5,23},{6,20},{7,21},{8,26},{9,... | collective-permute-start | bytes 221192 | tf_op jit(solution)/shard_map/ppermute | solution.py:20
  34.5 1.0 %collective-permute-done.23.from_y = bf16[2,48,384]{2,1,0:T(8,128)(2,1)S(1)} collective-permute-done((bf16[2,48,384]{2,1,0:T(8,128)(2,1)S(1)}, bf16[2,48,384]{2,1,0:T(8,128)(2,1)S(1)}, u32[]{:S(2)}, u32[]{:S(2)}) %collective-permute-start.23) | collective-permute-done | bytes 73760 | tf_op jit(solution)/shard_map/ppermute | solution.py:20
  35.5 1.2 %collective-permute-done.24.from_xy = bf16[2,48,384]{2,1,0:T(8,128)(2,1)S(1)} collective-permute-done((bf16[2,48,384]{2,1,0:T(8,128)(2,1)S(1)}, bf16[2,48,384]{2,1,0:T(8,128)(2,1)S(1)}, u32[]{:S(2)}, u32[]{:S(2)}) %collective-permute-start.24) | collective-permute-done | bytes 73760 | tf_op jit(solution)/shard_map/ppermute | solution.py:20
  36.7 0.1 shard_map.87
  36.8 0.5 %collective-permute-start.27 = (bf16[48,384]{1,0:T(8,128)(2,1)S(1)}, bf16[48,384]{1,0:T(8,128)(2,1)S(1)}, u32[]{:S(2)}, u32[]{:S(2)}) collective-permute-start(bf16[48,384]{1,0:T(8,128)(2,1)S(1)} %get-tuple-element.45), channel_id=1, source_target_pairs={{0,5},{1,4},{2,7},{3,6},{4,1},{5,0},{6,3},{7,2},{8,13},{9,12},{10,... | collective-permute-start | bytes 110600 | tf_op jit(solution)/shard_map/ppermute | solution.py:20
  37.3 1.6 %collective-permute-done.19.from_y = bf16[2,48,384]{2,1,0:T(8,128)(2,1)S(1)} collective-permute-done((bf16[2,48,384]{2,1,0:T(8,128)(2,1)S(1)}, bf16[2,48,384]{2,1,0:T(8,128)(2,1)S(1)}, u32[]{:S(2)}, u32[]{:S(2)}) %collective-permute-start.19) | collective-permute-done | bytes 73760 | tf_op jit(solution)/shard_map/ppermute | solution.py:20
  38.9 0.0 collective-permute-done.20.from_xy
  38.9 0.0 collective-permute-done.18.from_x
  38.9 0.1 shard_map.84
  39.0 2.9 %collective-permute-start.25 = (bf16[48,384]{1,0:T(8,128)(2,1)S(1)}, bf16[48,384]{1,0:T(8,128)(2,1)S(1)}, u32[]{:S(2)}, u32[]{:S(2)}) collective-permute-start(bf16[48,384]{1,0:T(8,128)(2,1)S(1)} %get-tuple-element.43), channel_id=1, source_target_pairs={{0,13},{1,12},{2,15},{3,14},{4,9},{5,8},{6,11},{7,10},{8,5},{9,4},... | collective-permute-start | bytes 110600 | tf_op jit(solution)/shard_map/ppermute | solution.py:20
  41.9 0.4 collective-permute-start.26
  42.3 2.0 %collective-permute-done.25.refs_0_ = bf16[48,384]{1,0:T(8,128)(2,1)S(1)} collective-permute-done((bf16[48,384]{1,0:T(8,128)(2,1)S(1)}, bf16[48,384]{1,0:T(8,128)(2,1)S(1)}, u32[]{:S(2)}, u32[]{:S(2)}) %collective-permute-start.25) | collective-permute-done | bytes 36896 | tf_op jit(solution)/shard_map/ppermute | solution.py:20
  44.3 1.8 %collective-permute-done.26.refs_1_ = bf16[48,384]{1,0:T(8,128)(2,1)S(1)} collective-permute-done((bf16[48,384]{1,0:T(8,128)(2,1)S(1)}, bf16[48,384]{1,0:T(8,128)(2,1)S(1)}, u32[]{:S(2)}, u32[]{:S(2)}) %collective-permute-start.26) | collective-permute-done | bytes 36896 | tf_op jit(solution)/shard_map/ppermute | solution.py:20
  46.2 0.6 %shard_map.88 = (bf16[48,384]{1,0:T(8,128)(2,1)}, f32[2,2]{1,0:T(2,128)}) custom-call(f32[16,128]{1,0:T(8,128)S(1)} %get-tuple-element.34.load, f32[48,384]{1,0:T(8,128)S(1)} %get-tuple-element.42.keep, bf16[48,384]{1,0:T(8,128)(2,1)S(1)} %collective-permute-done.25.refs_0_, bf16[48,384]{1,0:T(8,128)(2,1)S(1)} %collective-permute-done.26.refs_1_, ...), custom_call_target="tpu_custom_call" | custom-call | tf_op jit(solution)/shard_map/pallas_call | solution.py:157
  (16 shorter events, 0.0 us)
Async XLA Ops:
  0.6 8.4 %copy-start.3 = (bf16[48,384]{1,0:T(8,128)(2,1)S(1)}, bf16[48,384]{1,0:T(8,128)(2,1)}, u32[]{:S(2)}) copy-start(bf16[48,384]{1,0:T(8,128)(2,1)} %refs_1_.1) | copy-start | bytes 110596
  0.6 21.0 %copy-start = (bf16[1,512,6144]{2,1,0:T(8,128)(2,1)S(1)}, bf16[1,512,6144]{2,1,0:T(8,128)(2,1)}, u32[]{:S(2)}) copy-start(bf16[1,512,6144]{2,1,0:T(8,128)(2,1)} %weights.1) | copy-start | bytes 18874372
  0.7 21.0 %copy-start.2 = (bf16[1,6144,512]{2,1,0:T(8,128)(2,1)S(1)}, bf16[1,6144,512]{2,1,0:T(8,128)(2,1)}, u32[]{:S(2)}) copy-start(bf16[1,6144,512]{2,1,0:T(8,128)(2,1)} %refs_9_.3) | copy-start | bytes 18874372
  0.7 21.0 %copy-start.1 = (bf16[1,6144,512]{2,1,0:T(8,128)(2,1)S(1)}, bf16[1,6144,512]{2,1,0:T(8,128)(2,1)}, u32[]{:S(2)}) copy-start(bf16[1,6144,512]{2,1,0:T(8,128)(2,1)} %refs_8_.3) | copy-start | bytes 18874372
  0.7 11.9 %collective-permute-start.1 = (bf16[48,384]{1,0:T(8,128)(2,1)}, bf16[48,384]{1,0:T(8,128)(2,1)S(1)}, u32[]{:S(2)}, u32[]{:S(2)}) collective-permute-start(bf16[48,384]{1,0:T(8,128)(2,1)} %refs_1_.1), channel_id=1, source_target_pairs={{0,13},{1,12},{2,15},{3,14},{4,9},{5,8},{6,11},{7,10},{8,5},{9,4},... | collective-permute-start | bytes 110600 | tf_op jit(solution)/shard_map/ppermute | solution.py:20
  5.3 7.6 %collective-permute-start = (bf16[48,384]{1,0:T(8,128)(2,1)}, bf16[48,384]{1,0:T(8,128)(2,1)S(1)}, u32[]{:S(2)}, u32[]{:S(2)}) collective-permute-start(bf16[48,384]{1,0:T(8,128)(2,1)} %refs_1_.1), channel_id=1, source_target_pairs={{0,9},{1,8},{2,11},{3,10},{4,13},{5,12},{6,15},{7,14},{8,1},{9,0},... | collective-permute-start | bytes 110600 | tf_op jit(solution)/shard_map/ppermute | solution.py:20
  5.3 3.8 %collective-permute-start.9 = (bf16[48,384]{1,0:T(8,128)(2,1)}, bf16[48,384]{1,0:T(8,128)(2,1)S(1)}, u32[]{:S(2)}, u32[]{:S(2)}) collective-permute-start(bf16[48,384]{1,0:T(8,128)(2,1)} %refs_1_.1), channel_id=1, source_target_pairs={{0,5},{1,4},{2,7},{3,6},{4,1},{5,0},{6,3},{7,2},{8,13},{9,12},{10,... | collective-permute-start | bytes 110600 | tf_op jit(solution)/shard_map/ppermute | solution.py:20
  9.0 6.3 %collective-permute-start.15 = (bf16[2,48,384]{2,1,0:T(8,128)(2,1)S(1)}, bf16[2,48,384]{2,1,0:T(8,128)(2,1)S(1)}, u32[]{:S(2)}, u32[]{:S(2)}) collective-permute-start(bf16[2,48,384]{2,1,0:T(8,128)(2,1)S(1)} %shard_map.80.refs_0_), channel_id=1, source_target_pairs={{0,18},{1,19},{2,16},{3,17},{4,22},{5,23},{6,20},{7,21},{8,26},{9,... | collective-permute-start | bytes 221192 | tf_op jit(solution)/shard_map/ppermute | solution.py:20
  11.5 5.1 %collective-permute-start.13 = (bf16[2,48,384]{2,1,0:T(8,128)(2,1)S(1)}, bf16[2,48,384]{2,1,0:T(8,128)(2,1)S(1)}, u32[]{:S(2)}, u32[]{:S(2)}) collective-permute-start(bf16[2,48,384]{2,1,0:T(8,128)(2,1)S(1)} %shard_map.80.refs_0_), channel_id=1, source_target_pairs={{0,16},{1,17},{2,18},{3,19},{4,20},{5,21},{6,22},{7,23},{8,24},{9,... | collective-permute-start | bytes 221192 | tf_op jit(solution)/shard_map/ppermute | solution.py:20
  12.1 6.0 %collective-permute-start.11 = (bf16[2,48,384]{2,1,0:T(8,128)(2,1)S(1)}, bf16[2,48,384]{2,1,0:T(8,128)(2,1)S(1)}, u32[]{:S(2)}, u32[]{:S(2)}) collective-permute-start(bf16[2,48,384]{2,1,0:T(8,128)(2,1)S(1)} %shard_map.80.refs_0_), channel_id=1, source_target_pairs={{0,2},{1,3},{2,0},{3,1},{4,6},{5,7},{6,4},{7,5},{8,10},{9,11},{10,... | collective-permute-start | bytes 221192 | tf_op jit(solution)/shard_map/ppermute | solution.py:20
  12.6 5.5 %collective-permute-start.10 = (bf16[2,48,384]{2,1,0:T(8,128)(2,1)S(1)}, bf16[2,48,384]{2,1,0:T(8,128)(2,1)S(1)}, u32[]{:S(2)}, u32[]{:S(2)}) collective-permute-start(bf16[2,48,384]{2,1,0:T(8,128)(2,1)S(1)} %shard_map.80.refs_0_), channel_id=1, source_target_pairs={{0,1},{1,0},{2,3},{3,2},{4,5},{5,4},{6,7},{7,6},{8,9},{9,8},{10,11... | collective-permute-start | bytes 221192 | tf_op jit(solution)/shard_map/ppermute | solution.py:20
  12.8 5.8 %collective-permute-start.7 = (bf16[2,48,384]{2,1,0:T(8,128)(2,1)S(1)}, bf16[2,48,384]{2,1,0:T(8,128)(2,1)S(1)}, u32[]{:S(2)}, u32[]{:S(2)}) collective-permute-start(bf16[2,48,384]{2,1,0:T(8,128)(2,1)S(1)} %shard_map.79.refs_0_), channel_id=1, source_target_pairs={{0,18},{1,19},{2,16},{3,17},{4,22},{5,23},{6,20},{7,21},{8,26},{9,... | collective-permute-start | bytes 221192 | tf_op jit(solution)/shard_map/ppermute | solution.py:20
  15.4 4.6 %collective-permute-start.5 = (bf16[2,48,384]{2,1,0:T(8,128)(2,1)S(1)}, bf16[2,48,384]{2,1,0:T(8,128)(2,1)S(1)}, u32[]{:S(2)}, u32[]{:S(2)}) collective-permute-start(bf16[2,48,384]{2,1,0:T(8,128)(2,1)S(1)} %shard_map.79.refs_0_), channel_id=1, source_target_pairs={{0,16},{1,17},{2,18},{3,19},{4,20},{5,21},{6,22},{7,23},{8,24},{9,... | collective-permute-start | bytes 221192 | tf_op jit(solution)/shard_map/ppermute | solution.py:20
  16.7 4.4 %collective-permute-start.3 = (bf16[2,48,384]{2,1,0:T(8,128)(2,1)S(1)}, bf16[2,48,384]{2,1,0:T(8,128)(2,1)S(1)}, u32[]{:S(2)}, u32[]{:S(2)}) collective-permute-start(bf16[2,48,384]{2,1,0:T(8,128)(2,1)S(1)} %shard_map.79.refs_0_), channel_id=1, source_target_pairs={{0,2},{1,3},{2,0},{3,1},{4,6},{5,7},{6,4},{7,5},{8,10},{9,11},{10,... | collective-permute-start | bytes 221192 | tf_op jit(solution)/shard_map/ppermute | solution.py:20
  18.1 3.0 %collective-permute-start.16 = (bf16[2,48,384]{2,1,0:T(8,128)(2,1)S(1)}, bf16[2,48,384]{2,1,0:T(8,128)(2,1)S(1)}, u32[]{:S(2)}, u32[]{:S(2)}) collective-permute-start(bf16[2,48,384]{2,1,0:T(8,128)(2,1)S(1)} %collective-permute-done.15.refs_6_), channel_id=1, source_target_pairs={{0,1},{1,0},{2,3},{3,2},{4,5},{5,4},{6,7},{7,6},{8,9},{9,8},{10,11... | collective-permute-start | bytes 221192 | tf_op jit(solution)/shard_map/ppermute | solution.py:20
  18.1 3.5 %collective-permute-start.14 = (bf16[2,48,384]{2,1,0:T(8,128)(2,1)S(1)}, bf16[2,48,384]{2,1,0:T(8,128)(2,1)S(1)}, u32[]{:S(2)}, u32[]{:S(2)}) collective-permute-start(bf16[2,48,384]{2,1,0:T(8,128)(2,1)S(1)} %collective-permute-done.13.refs_4_), channel_id=1, source_target_pairs={{0,1},{1,0},{2,3},{3,2},{4,5},{5,4},{6,7},{7,6},{8,9},{9,8},{10,11... | collective-permute-start | bytes 221192 | tf_op jit(solution)/shard_map/ppermute | solution.py:20
  18.6 3.0 %collective-permute-start.12 = (bf16[2,48,384]{2,1,0:T(8,128)(2,1)S(1)}, bf16[2,48,384]{2,1,0:T(8,128)(2,1)S(1)}, u32[]{:S(2)}, u32[]{:S(2)}) collective-permute-start(bf16[2,48,384]{2,1,0:T(8,128)(2,1)S(1)} %collective-permute-done.11.refs_2_), channel_id=1, source_target_pairs={{0,1},{1,0},{2,3},{3,2},{4,5},{5,4},{6,7},{7,6},{8,9},{9,8},{10,11... | collective-permute-start | bytes 221192 | tf_op jit(solution)/shard_map/ppermute | solution.py:20
  19.9 2.9 %collective-permute-start.2 = (bf16[2,48,384]{2,1,0:T(8,128)(2,1)S(1)}, bf16[2,48,384]{2,1,0:T(8,128)(2,1)S(1)}, u32[]{:S(2)}, u32[]{:S(2)}) collective-permute-start(bf16[2,48,384]{2,1,0:T(8,128)(2,1)S(1)} %shard_map.79.refs_0_), channel_id=1, source_target_pairs={{0,1},{1,0},{2,3},{3,2},{4,5},{5,4},{6,7},{7,6},{8,9},{9,8},{10,11... | collective-permute-start | bytes 221192 | tf_op jit(solution)/shard_map/ppermute | solution.py:20
  21.1 1.8 %collective-permute-start.8 = (bf16[2,48,384]{2,1,0:T(8,128)(2,1)S(1)}, bf16[2,48,384]{2,1,0:T(8,128)(2,1)S(1)}, u32[]{:S(2)}, u32[]{:S(2)}) collective-permute-start(bf16[2,48,384]{2,1,0:T(8,128)(2,1)S(1)} %collective-permute-done.7.refs_6_), channel_id=1, source_target_pairs={{0,1},{1,0},{2,3},{3,2},{4,5},{5,4},{6,7},{7,6},{8,9},{9,8},{10,11... | collective-permute-start | bytes 221192 | tf_op jit(solution)/shard_map/ppermute | solution.py:20
  21.1 1.8 %collective-permute-start.6 = (bf16[2,48,384]{2,1,0:T(8,128)(2,1)S(1)}, bf16[2,48,384]{2,1,0:T(8,128)(2,1)S(1)}, u32[]{:S(2)}, u32[]{:S(2)}) collective-permute-start(bf16[2,48,384]{2,1,0:T(8,128)(2,1)S(1)} %collective-permute-done.5.refs_4_), channel_id=1, source_target_pairs={{0,1},{1,0},{2,3},{3,2},{4,5},{5,4},{6,7},{7,6},{8,9},{9,8},{10,11... | collective-permute-start | bytes 221192 | tf_op jit(solution)/shard_map/ppermute | solution.py:20
  21.6 1.3 %collective-permute-start.4 = (bf16[2,48,384]{2,1,0:T(8,128)(2,1)S(1)}, bf16[2,48,384]{2,1,0:T(8,128)(2,1)S(1)}, u32[]{:S(2)}, u32[]{:S(2)}) collective-permute-start(bf16[2,48,384]{2,1,0:T(8,128)(2,1)S(1)} %collective-permute-done.3.refs_2_), channel_id=1, source_target_pairs={{0,1},{1,0},{2,3},{3,2},{4,5},{5,4},{6,7},{7,6},{8,9},{9,8},{10,11... | collective-permute-start | bytes 221192 | tf_op jit(solution)/shard_map/ppermute | solution.py:20
  24.7 4.1 %copy-start.4 = (s32[48,2]{0,1:T(2,128)S(1)}, s32[48,2]{0,1:T(2,128)}, u32[]{:S(2)}) copy-start(s32[48,2]{0,1:T(2,128)} %param.7) | copy-start | bytes 1156
  24.7 4.0 %copy-start.5 = (s32[48,2]{0,1:T(2,128)S(1)}, s32[48,2]{0,1:T(2,128)}, u32[]{:S(2)}) copy-start(s32[48,2]{0,1:T(2,128)} %param.8) | copy-start | bytes 1156
  25.4 1.7 %collective-permute-start.21 = (bf16[2,2,2,48,384]{4,3,2,1,0:T(8,128)(2,1)S(1)}, bf16[2,2,2,48,384]{4,3,2,1,0:T(8,128)(2,1)S(1)}, u32[]{:S(2)}, u32[]{:S(2)}) collective-permute-start(bf16[2,2,2,48,384]{4,3,2,1,0:T(8,128)(2,1)S(1)} %get-tuple-element.37), channel_id=1, source_target_pairs={{0,1},{1,0},{2,3},{3,2},{4,5},{5,4},{6,7},{7,6},{8,9},{9,8},{10,11... | collective-permute-start | bytes 884744 | tf_op jit(solution)/shard_map/ppermute | solution.py:20
  25.9 3.0 %collective-permute-start.17 = (bf16[2,2,2,48,384]{4,3,2,1,0:T(8,128)(2,1)S(1)}, bf16[2,2,2,48,384]{4,3,2,1,0:T(8,128)(2,1)S(1)}, u32[]{:S(2)}, u32[]{:S(2)}) collective-permute-start(bf16[2,2,2,48,384]{4,3,2,1,0:T(8,128)(2,1)S(1)} %get-tuple-element.28), channel_id=1, source_target_pairs={{0,1},{1,0},{2,3},{3,2},{4,5},{5,4},{6,7},{7,6},{8,9},{9,8},{10,11... | collective-permute-start | bytes 884744 | tf_op jit(solution)/shard_map/ppermute | solution.py:20
  27.2 6.1 %collective-permute-start.22 = (bf16[96,384]{1,0:T(8,128)(2,1)S(1)}, bf16[96,384]{1,0:T(8,128)(2,1)S(1)}, u32[]{:S(2)}, u32[]{:S(2)}) collective-permute-start(bf16[96,384]{1,0:T(8,128)(2,1)S(1)} %get-tuple-element.39), channel_id=1, source_target_pairs={{0,16},{1,17},{2,18},{3,19},{4,20},{5,21},{6,22},{7,23},{8,24},{9,... | collective-permute-start | bytes 221192 | tf_op jit(solution)/shard_map/ppermute | solution.py:20
  28.9 10.0 %collective-permute-start.18 = (bf16[112,384]{1,0:T(8,128)(2,1)S(1)}, bf16[112,384]{1,0:T(8,128)(2,1)S(1)}, u32[]{:S(2)}, u32[]{:S(2)}) collective-permute-start(bf16[112,384]{1,0:T(8,128)(2,1)S(1)} %get-tuple-element.31), channel_id=1, source_target_pairs={{0,16},{1,17},{2,18},{3,19},{4,20},{5,21},{6,22},{7,23},{8,24},{9,... | collective-permute-start | bytes 258056 | tf_op jit(solution)/shard_map/ppermute | solution.py:20
  29.5 6.0 %collective-permute-start.23 = (bf16[2,48,384]{2,1,0:T(8,128)(2,1)S(1)}, bf16[2,48,384]{2,1,0:T(8,128)(2,1)S(1)}, u32[]{:S(2)}, u32[]{:S(2)}) collective-permute-start(bf16[2,48,384]{2,1,0:T(8,128)(2,1)S(1)} %get-tuple-element.40), channel_id=1, source_target_pairs={{0,2},{1,3},{2,0},{3,1},{4,6},{5,7},{6,4},{7,5},{8,10},{9,11},{10,... | collective-permute-start | bytes 221192 | tf_op jit(solution)/shard_map/ppermute | solution.py:20
  30.9 5.7 %collective-permute-start.24 = (bf16[2,48,384]{2,1,0:T(8,128)(2,1)S(1)}, bf16[2,48,384]{2,1,0:T(8,128)(2,1)S(1)}, u32[]{:S(2)}, u32[]{:S(2)}) collective-permute-start(bf16[2,48,384]{2,1,0:T(8,128)(2,1)S(1)} %get-tuple-element.41), channel_id=1, source_target_pairs={{0,18},{1,19},{2,16},{3,17},{4,22},{5,23},{6,20},{7,21},{8,26},{9,... | collective-permute-start | bytes 221192 | tf_op jit(solution)/shard_map/ppermute | solution.py:20
  32.5 6.4 %collective-permute-start.19 = (bf16[2,48,384]{2,1,0:T(8,128)(2,1)S(1)}, bf16[2,48,384]{2,1,0:T(8,128)(2,1)S(1)}, u32[]{:S(2)}, u32[]{:S(2)}) collective-permute-start(bf16[2,48,384]{2,1,0:T(8,128)(2,1)S(1)} %get-tuple-element.32), channel_id=1, source_target_pairs={{0,2},{1,3},{2,0},{3,1},{4,6},{5,7},{6,4},{7,5},{8,10},{9,11},{10,... | collective-permute-start | bytes 221192 | tf_op jit(solution)/shard_map/ppermute | solution.py:20
  33.2 5.7 %collective-permute-start.20 = (bf16[2,48,384]{2,1,0:T(8,128)(2,1)S(1)}, bf16[2,48,384]{2,1,0:T(8,128)(2,1)S(1)}, u32[]{:S(2)}, u32[]{:S(2)}) collective-permute-start(bf16[2,48,384]{2,1,0:T(8,128)(2,1)S(1)} %get-tuple-element.33), channel_id=1, source_target_pairs={{0,18},{1,19},{2,16},{3,17},{4,22},{5,23},{6,20},{7,21},{8,26},{9,... | collective-permute-start | bytes 221192 | tf_op jit(solution)/shard_map/ppermute | solution.py:20
  36.8 5.5 %collective-permute-start.27 = (bf16[48,384]{1,0:T(8,128)(2,1)S(1)}, bf16[48,384]{1,0:T(8,128)(2,1)S(1)}, u32[]{:S(2)}, u32[]{:S(2)}) collective-permute-start(bf16[48,384]{1,0:T(8,128)(2,1)S(1)} %get-tuple-element.45), channel_id=1, source_target_pairs={{0,5},{1,4},{2,7},{3,6},{4,1},{5,0},{6,3},{7,2},{8,13},{9,12},{10,... | collective-permute-start | bytes 110600 | tf_op jit(solution)/shard_map/ppermute | solution.py:20
  39.0 5.3 %collective-permute-start.25 = (bf16[48,384]{1,0:T(8,128)(2,1)S(1)}, bf16[48,384]{1,0:T(8,128)(2,1)S(1)}, u32[]{:S(2)}, u32[]{:S(2)}) collective-permute-start(bf16[48,384]{1,0:T(8,128)(2,1)S(1)} %get-tuple-element.43), channel_id=1, source_target_pairs={{0,13},{1,12},{2,15},{3,14},{4,9},{5,8},{6,11},{7,10},{8,5},{9,4},... | collective-permute-start | bytes 110600 | tf_op jit(solution)/shard_map/ppermute | solution.py:20
  41.9 4.3 %collective-permute-start.26 = (bf16[48,384]{1,0:T(8,128)(2,1)S(1)}, bf16[48,384]{1,0:T(8,128)(2,1)S(1)}, u32[]{:S(2)}, u32[]{:S(2)}) collective-permute-start(bf16[48,384]{1,0:T(8,128)(2,1)S(1)} %get-tuple-element.44), channel_id=1, source_target_pairs={{0,9},{1,8},{2,11},{3,10},{4,13},{5,12},{6,15},{7,14},{8,1},{9,0},... | collective-permute-start | bytes 110600 | tf_op jit(solution)/shard_map/ppermute | solution.py:20
